TPU v7x, 32 devices: a whole 2x2x4 slice. The times are simulated.
32 devices in a mesh: modes: 8 (over z, y), cheb: 4 (over x, core).
Axes of the slice: x: 2, y: 2, z: 4, core: 2. Of those that a mesh axis runs over, the one named last changes fastest.
Arguments:
- start: float32 [2, 2, 2048, 256], P(None, None, ('modes', 'cheb')), may hold values from -45 to 45
- forcing: float32 [2, 2, 2048, 256], P(None, None, ('modes', 'cheb')), may hold values from -45 to 45
- taus: float32 [2048, 256, 256], P(('modes', 'cheb')), may hold values from -5 to 5
Outputs:
- solution: float32 [2, 2, 2048, 256], P(None, None, ('modes', 'cheb'))
All inputs are finite; a program needn't handle non-finite values.
Results may differ from a plain program's by a relative error of at most 0.0002.
Values sent between devices are 32-bit elements; how exact they have to be, the bound alone decides.
No kernel may reach another device: no remote copies, remote signals or barrier semaphores. Data moves between devices by JAX's collectives and lax.ppermute only.
A program may use at most 128 MiB of HBM per device.

v0:
```python
import math

import jax
import jax.numpy as jnp
from jax import lax
from jax.sharding import PartitionSpec as P

NEWTON = 2
KRYLOV = 3


HIGH = lax.Precision.HIGHEST
STRENGTH = 0.1


def cheb_rows(degree_count):
    degree = jnp.arange(degree_count, dtype=jnp.int32)[:, None]
    node = 2 * jnp.arange(degree_count, dtype=jnp.int32)[None, :] + 1
    turns = degree * node % (4 * degree_count)
    return jnp.cos(2.0 * math.pi / (4 * degree_count) * turns.astype(jnp.float32))


def phase_table(row_count, col_count, period):
    row_index = jnp.arange(row_count, dtype=jnp.int32)[:, None]
    col_index = jnp.arange(col_count, dtype=jnp.int32)[None, :]
    turns = row_index * col_index % period
    angle = 2.0 * math.pi / period * turns.astype(jnp.float32)
    return (jnp.cos(angle), jnp.sin(angle))


def inverse_points(spectrum, outer_len, inner_len, factor):
    half_inner = inner_len // 2
    lead_shape = spectrum.shape[:-3]
    row_count = spectrum.shape[-2]
    weights = jnp.where(jnp.arange(outer_len * half_inner) == 0, 1.0, 2.0).astype(jnp.float32)
    real_part = (spectrum[..., 0, :, :] * weights).reshape(
        lead_shape + (row_count, half_inner, outer_len)
    )
    imag_part = (spectrum[..., 1, :, :] * weights).reshape(
        lead_shape + (row_count, half_inner, outer_len)
    )
    section_cos, section_sin = phase_table(inner_len, half_inner, inner_len)
    upper_real = jnp.einsum(
        "jq,...yqa->...yja", section_cos, real_part, precision=HIGH
    ) - jnp.einsum("jq,...yqa->...yja", section_sin, imag_part, precision=HIGH)
    upper_imag = jnp.einsum(
        "jq,...yqa->...yja", section_sin, real_part, precision=HIGH
    ) + jnp.einsum("jq,...yqa->...yja", section_cos, imag_part, precision=HIGH)
    twist_cos, twist_sin = phase_table(inner_len, outer_len, inner_len * outer_len)
    turned_real = upper_real * twist_cos - upper_imag * twist_sin
    turned_imag = upper_real * twist_sin + upper_imag * twist_cos
    final_cos, final_sin = phase_table(outer_len, outer_len, outer_len)
    points = jnp.einsum("ta,...yja->...ytj", final_cos, turned_real, precision=HIGH) - jnp.einsum(
        "ta,...yja->...ytj", final_sin, turned_imag, precision=HIGH
    )
    return points.reshape(lead_shape + (row_count, outer_len * inner_len)) * factor


def forward_modes(points, outer_len, inner_len, factor):
    half_inner = inner_len // 2
    lead_shape = points.shape[:-2]
    row_count = points.shape[-2]
    gridded = points.reshape(lead_shape + (row_count, outer_len, inner_len))
    first_cos, first_sin = phase_table(outer_len, outer_len, outer_len)
    part_real = jnp.einsum("at,...ytj->...yaj", first_cos, gridded, precision=HIGH)
    part_imag = -jnp.einsum("at,...ytj->...yaj", first_sin, gridded, precision=HIGH)
    twist_cos, twist_sin = phase_table(outer_len, inner_len, inner_len * outer_len)
    turned_real = part_real * twist_cos + part_imag * twist_sin
    turned_imag = part_imag * twist_cos - part_real * twist_sin
    last_cos, last_sin = phase_table(half_inner, inner_len, inner_len)
    coef_real = jnp.einsum("qj,...yaj->...yqa", last_cos, turned_real, precision=HIGH) + jnp.einsum(
        "qj,...yaj->...yqa", last_sin, turned_imag, precision=HIGH
    )
    coef_imag = jnp.einsum("qj,...yaj->...yqa", last_cos, turned_imag, precision=HIGH) - jnp.einsum(
        "qj,...yaj->...yqa", last_sin, turned_real, precision=HIGH
    )
    coef_real = coef_real.reshape(lead_shape + (row_count, half_inner * outer_len))
    coef_imag = coef_imag.reshape(lead_shape + (row_count, half_inner * outer_len))
    return jnp.stack([coef_real, coef_imag], axis=-3) * factor


def least_squares(hessen, beta_norm):
    steps_count = len(hessen)
    matrix = [
        [hessen[col_index][:, row_index] for row_index in range(col_index + 2)]
        for col_index in range(steps_count)
    ]
    target = [beta_norm] + [jnp.zeros_like(beta_norm) for row_index in range(steps_count)]
    cosines = []
    sines_list = []
    for col_index in range(steps_count):
        column = matrix[col_index]
        for row_index in range(col_index):
            upper_entry = (
                cosines[row_index] * column[row_index]
                + sines_list[row_index] * column[row_index + 1]
            )
            lower_entry = (
                cosines[row_index] * column[row_index + 1]
                - sines_list[row_index] * column[row_index]
            )
            column[row_index] = upper_entry
            column[row_index + 1] = lower_entry
        radius = jnp.sqrt(
            column[col_index] * column[col_index] + column[col_index + 1] * column[col_index + 1]
        )
        cosines.append(column[col_index] / radius)
        sines_list.append(column[col_index + 1] / radius)
        column[col_index] = radius
        target[col_index + 1] = -sines_list[col_index] * target[col_index]
        target[col_index] = cosines[col_index] * target[col_index]
    solved = [None] * steps_count
    for row_index in reversed(range(steps_count)):
        partial_sum = target[row_index]
        for col_index in range(row_index + 1, steps_count):
            partial_sum = partial_sum - matrix[col_index][row_index] * solved[col_index]
        solved[row_index] = partial_sum / matrix[row_index][row_index]
    return solved


def shards(start, forcing, taus):
    group_size = lax.axis_size(("modes", "cheb"))
    local_modes = start.shape[2]
    degrees = start.shape[3]
    total_modes = local_modes * group_size
    points_count = 2 * total_modes
    outer_len = 2 ** ((points_count.bit_length() - 1) // 2)
    inner_len = points_count // outer_len
    spread = 1.0 / math.sqrt(total_modes * degrees)
    gather_factor = math.sqrt(total_modes * degrees) / points_count
    cheb_table = cheb_rows(degrees)
    offset = lax.axis_index(("modes", "cheb")) * local_modes
    wavenumber = (
        16.0 * (offset + jnp.arange(local_modes, dtype=jnp.int32)).astype(jnp.float32) / total_modes
    )
    tau_keep = (jnp.arange(degrees) < degrees - 2).astype(jnp.float32)
    coef_weights = jnp.where(jnp.arange(degrees) == 0, 1.0, 2.0).astype(jnp.float32) / degrees

    def move_out(stacked):
        return lax.all_to_all(stacked, ("modes", "cheb"), split_axis=3, concat_axis=4, tiled=True)

    def move_back(spectrum):
        return lax.all_to_all(spectrum, ("modes", "cheb"), split_axis=3, concat_axis=2, tiled=True)

    def to_points(coefs):
        values = jnp.einsum("brkn,ni->brik", coefs, cheb_table, precision=HIGH)
        slopes = jnp.stack([-wavenumber * values[:, 1], wavenumber * values[:, 0]], axis=1)
        spectrum = move_out(jnp.stack([values, slopes], axis=0))
        grid_pair = inverse_points(spectrum, outer_len, inner_len, spread)
        return (grid_pair[0], grid_pair[1])

    def to_coefficients(points):
        spectrum = forward_modes(points, outer_len, inner_len, gather_factor)
        slab_vals = move_back(spectrum)
        return jnp.einsum("brik,ni->brkn", slab_vals, cheb_table, precision=HIGH) * coef_weights

    def precondition(coefs):
        return jnp.einsum("kam,brkm->brka", taus, coefs * tau_keep, precision=HIGH)

    iterate = start
    for newton_step in range(NEWTON):
        base_points, base_slopes = to_points(iterate)
        residual = iterate + precondition(
            to_coefficients(STRENGTH * base_points * base_slopes) - forcing
        )
        squared = lax.psum(jnp.sum(residual * residual, axis=(1, 2, 3)), ("modes", "cheb"))
        beta_norm = jnp.sqrt(squared)
        krylov_basis = [-residual / beta_norm[:, None, None, None]]
        hessen = []
        for column in range(KRYLOV):
            probe_points, probe_slopes = to_points(krylov_basis[column])
            product = STRENGTH * (base_points * probe_slopes + probe_points * base_slopes)
            applied = krylov_basis[column] + precondition(to_coefficients(product))
            local_dots = jnp.stack(
                [jnp.sum(vector * applied, axis=(1, 2, 3)) for vector in krylov_basis], axis=1
            )
            local_square = jnp.sum(applied * applied, axis=(1, 2, 3))
            projections, square = lax.psum((local_dots, local_square), ("modes", "cheb"))
            remove_applied = applied
            for index, remove_vector in enumerate(krylov_basis):
                remove_applied = (
                    remove_applied - projections[:, index][:, None, None, None] * remove_vector
                )
            applied = remove_applied
            length = jnp.sqrt(square - jnp.sum(projections * projections, axis=1))
            hessen.append(jnp.concatenate([projections, length[:, None]], axis=1))
            krylov_basis.append(applied / length[:, None, None, None])
        solved = least_squares(hessen, beta_norm)
        for column in range(KRYLOV):
            iterate = iterate + solved[column][:, None, None, None] * krylov_basis[column]
    return iterate


def solution(mesh):
    return jax.shard_map(
        shards,
        mesh=mesh,
        in_specs=(
            P(None, None, ("modes", "cheb"), None),
            P(None, None, ("modes", "cheb"), None),
            P(("modes", "cheb"), None, None),
        ),
        out_specs=P(None, None, ("modes", "cheb"), None),
        check_vma=False,
    )
```

profile of v0, /device:TPU:0, one launch (start us, length us, event | category | flops | bytes accessed | tf_op | source)
XLA Modules:
  0.0 1151.1 jit_solution(514577233461936301)
XLA Ops:
  5.2 7.6 all-to-all-start
  13.3 14.9 %all-to-all-done = f32[32,1,4096]{2,1,0:T(1,128)S(1)} async-done(((f32[32,1,4096]{2,1,0:T(1,128)}), f32[32,1,4096]{2,1,0:T(1,128)S(1)}, u32[]{:S(2)}, u32[]{:S(2)}) %all-to-all-start) | async-done | bytes 524320 | tf_op jit(solution)/shard_map/all_to_all | solution.py:140
  52.4 7.9 reshape.338
  63.4 10.5 all-to-all-done.1
  75.2 7.6 reshape.339
  89.0 17.4 %fusion.14 = f32[64,2,2,256]{3,2,1,0:T(2,128)S(1)} fusion(f32[64,256,256]{2,1,0:T(8,128)} %param.5, f32[2,2,64,256]{3,2,1,0:T(8,128)S(1)} %fusion.73), kind=kOutput, calls=%fused_computation.14 | convolution fusion | flops 201326592 | bytes 17301504 | tf_op jit(solution)/shard_map/kam,brkm->brka/dot_general | solution.py:158
  106.6 38.5 %psum.98 = f32[2]{0:T(128)S(1)} all-reduce(f32[2]{0:T(128)S(1)} %multiply_reduce_fusion.19), channel_id=1, replica_groups=mesh['modes'=8,'cheb'=4] {'modes','cheb'}, use_global_device_ids=true, to_apply=%region_1.2 | all-reduce | flops 2 | bytes 16 | tf_op jit(solution)/shard_map/psum | solution.py:166
  148.7 19.1 %all_to_all.288 = f32[32,1,4096]{2,1,0:T(1,128)S(1)} all-to-all(f32[32,1,4096]{2,1,0:T(1,128)S(1)} %reshape.340), channel_id=1, replica_groups=mesh['modes'=8,'cheb'=4] {'modes','cheb'}, dimensions={0} | all-to-all | bytes 1048576 | tf_op jit(solution)/shard_map/all_to_all | solution.py:140
  196.1 7.2 reshape.342
  203.3 13.5 %all_to_all.289 = f32[32,1,2048]{2,1,0:T(1,128)S(1)} all-to-all(f32[32,1,2048]{2,1,0:T(1,128)S(1)} %reshape.342), channel_id=1, replica_groups=mesh['modes'=8,'cheb'=4] {'modes','cheb'}, dimensions={0} | all-to-all | bytes 524288 | tf_op jit(solution)/shard_map/all_to_all | solution.py:143
  218.0 7.6 reshape.343
  231.8 17.4 %fusion.12 = f32[64,2,2,256]{3,2,1,0:T(2,128)S(1)} fusion(f32[64,256,256]{2,1,0:T(8,128)} %param.5, f32[2,2,64,256]{3,2,1,0:T(8,128)S(1)} %fusion.74), kind=kOutput, calls=%fused_computation.12 | convolution fusion | flops 201326592 | bytes 17301504 | tf_op jit(solution)/shard_map/kam,brkm->brka/dot_general | solution.py:158
  249.4 38.6 %all-reduce.5 = (f32[2]{0:T(128)S(1)}, f32[2,1]{0,1:T(1,128)S(1)}) all-reduce(f32[2]{0:T(128)S(1)} %get-tuple-element.22, f32[2,1]{0,1:T(1,128)S(1)} %bitcast.1009), channel_id=1, replica_groups=mesh['modes'=8,'cheb'=4] {'modes','cheb'}, use_global_device_ids=true, to_apply=%region_5.6 | all-reduce | flops 4 | bytes 32 | tf_op jit(solution)/shard_map/psum | solution.py:178
  291.5 19.1 %all_to_all.290 = f32[32,1,4096]{2,1,0:T(1,128)S(1)} all-to-all(f32[32,1,4096]{2,1,0:T(1,128)S(1)} %reshape.344), channel_id=1, replica_groups=mesh['modes'=8,'cheb'=4] {'modes','cheb'}, dimensions={0} | all-to-all | bytes 1048576 | tf_op jit(solution)/shard_map/all_to_all | solution.py:140
  338.9 7.2 reshape.346
  346.1 13.5 %all_to_all.291 = f32[32,1,2048]{2,1,0:T(1,128)S(1)} all-to-all(f32[32,1,2048]{2,1,0:T(1,128)S(1)} %reshape.346), channel_id=1, replica_groups=mesh['modes'=8,'cheb'=4] {'modes','cheb'}, dimensions={0} | all-to-all | bytes 524288 | tf_op jit(solution)/shard_map/all_to_all | solution.py:143
  360.9 7.6 reshape.347
  374.7 17.4 %fusion.10 = f32[64,2,2,256]{3,2,1,0:T(2,128)S(1)} fusion(f32[64,256,256]{2,1,0:T(8,128)} %param.5, f32[2,2,64,256]{3,2,1,0:T(8,128)S(1)} %fusion.75), kind=kOutput, calls=%fused_computation.10 | convolution fusion | flops 201326592 | bytes 17301504 | tf_op jit(solution)/shard_map/kam,brkm->brka/dot_general | solution.py:158
  392.3 38.6 %all-reduce.4 = (f32[2]{0:T(128)S(1)}, f32[2,2]{0,1:T(2,128)S(1)}) all-reduce(f32[2]{0:T(128)S(1)} %get-tuple-element.19, f32[2,2]{0,1:T(2,128)S(1)} %pad_maximum_fusion.10), channel_id=1, replica_groups=mesh['modes'=8,'cheb'=4] {'modes','cheb'}, use_global_device_ids=true, to_apply=%region_10.11 | all-reduce | flops 6 | bytes 48 | tf_op jit(solution)/shard_map/psum | solution.py:178
  434.5 19.1 %all_to_all.292 = f32[32,1,4096]{2,1,0:T(1,128)S(1)} all-to-all(f32[32,1,4096]{2,1,0:T(1,128)S(1)} %reshape.348), channel_id=1, replica_groups=mesh['modes'=8,'cheb'=4] {'modes','cheb'}, dimensions={0} | all-to-all | bytes 1048576 | tf_op jit(solution)/shard_map/all_to_all | solution.py:140
  481.9 7.3 reshape.350
  489.2 13.5 %all_to_all.293 = f32[32,1,2048]{2,1,0:T(1,128)S(1)} all-to-all(f32[32,1,2048]{2,1,0:T(1,128)S(1)} %reshape.350), channel_id=1, replica_groups=mesh['modes'=8,'cheb'=4] {'modes','cheb'}, dimensions={0} | all-to-all | bytes 524288 | tf_op jit(solution)/shard_map/all_to_all | solution.py:143
  503.9 7.6 reshape.351
  517.7 17.4 %fusion.8 = f32[64,2,2,256]{3,2,1,0:T(2,128)S(1)} fusion(f32[64,256,256]{2,1,0:T(8,128)} %param.5, f32[2,2,64,256]{3,2,1,0:T(8,128)S(1)} %fusion.76), kind=kOutput, calls=%fused_computation.8 | convolution fusion | flops 201326592 | bytes 17301504 | tf_op jit(solution)/shard_map/kam,brkm->brka/dot_general | solution.py:158
  535.4 38.6 %all-reduce.3 = (f32[2]{0:T(128)S(1)}, f32[2,3]{0,1:T(4,128)S(1)}) all-reduce(f32[2]{0:T(128)S(1)} %get-tuple-element.16, f32[2,3]{0,1:T(4,128)S(1)} %pad_maximum_fusion.8), channel_id=1, replica_groups=mesh['modes'=8,'cheb'=4] {'modes','cheb'}, use_global_device_ids=true, to_apply=%region_17.18 | all-reduce | flops 8 | bytes 64 | tf_op jit(solution)/shard_map/psum | solution.py:178
  578.6 19.1 %all_to_all.294 = f32[32,1,4096]{2,1,0:T(1,128)S(1)} all-to-all(f32[32,1,4096]{2,1,0:T(1,128)S(1)} %reshape.352), channel_id=1, replica_groups=mesh['modes'=8,'cheb'=4] {'modes','cheb'}, dimensions={0} | all-to-all | bytes 1048576 | tf_op jit(solution)/shard_map/all_to_all | solution.py:140
  621.4 7.2 reshape.354
  628.6 13.5 %all_to_all.295 = f32[32,1,2048]{2,1,0:T(1,128)S(1)} all-to-all(f32[32,1,2048]{2,1,0:T(1,128)S(1)} %reshape.354), channel_id=1, replica_groups=mesh['modes'=8,'cheb'=4] {'modes','cheb'}, dimensions={0} | all-to-all | bytes 524288 | tf_op jit(solution)/shard_map/all_to_all | solution.py:143
  643.3 7.6 reshape.355
  657.1 17.4 %fusion.6 = f32[64,2,2,256]{3,2,1,0:T(2,128)S(1)} fusion(f32[64,256,256]{2,1,0:T(8,128)} %param.5, f32[2,2,64,256]{3,2,1,0:T(8,128)S(1)} %fusion.78), kind=kOutput, calls=%fused_computation.6 | convolution fusion | flops 201326592 | bytes 17301504 | tf_op jit(solution)/shard_map/kam,brkm->brka/dot_general | solution.py:158
  674.7 38.5 %psum.105 = f32[2]{0:T(128)S(1)} all-reduce(f32[2]{0:T(128)S(1)} %multiply_reduce_fusion.9), channel_id=1, replica_groups=mesh['modes'=8,'cheb'=4] {'modes','cheb'}, use_global_device_ids=true, to_apply=%region_20.21 | all-reduce | flops 2 | bytes 16 | tf_op jit(solution)/shard_map/psum | solution.py:166
  716.8 19.1 %all_to_all.296 = f32[32,1,4096]{2,1,0:T(1,128)S(1)} all-to-all(f32[32,1,4096]{2,1,0:T(1,128)S(1)} %reshape.356), channel_id=1, replica_groups=mesh['modes'=8,'cheb'=4] {'modes','cheb'}, dimensions={0} | all-to-all | bytes 1048576 | tf_op jit(solution)/shard_map/all_to_all | solution.py:140
  771.4 13.5 %all_to_all.297 = f32[32,1,2048]{2,1,0:T(1,128)S(1)} all-to-all(f32[32,1,2048]{2,1,0:T(1,128)S(1)} %reshape.358), channel_id=1, replica_groups=mesh['modes'=8,'cheb'=4] {'modes','cheb'}, dimensions={0} | all-to-all | bytes 524288 | tf_op jit(solution)/shard_map/all_to_all | solution.py:143
  786.1 7.6 reshape.359
  799.9 17.4 %fusion.4 = f32[64,2,2,256]{3,2,1,0:T(2,128)S(1)} fusion(f32[64,256,256]{2,1,0:T(8,128)} %param.5, f32[2,2,64,256]{3,2,1,0:T(8,128)S(1)} %fusion.79), kind=kOutput, calls=%fused_computation.4 | convolution fusion | flops 201326592 | bytes 17301504 | tf_op jit(solution)/shard_map/kam,brkm->brka/dot_general | solution.py:158
  817.5 38.6 %all-reduce.2 = (f32[2]{0:T(128)S(1)}, f32[2,1]{0,1:T(1,128)S(1)}) all-reduce(f32[2]{0:T(128)S(1)} %get-tuple-element.13, f32[2,1]{0,1:T(1,128)S(1)} %bitcast.1010), channel_id=1, replica_groups=mesh['modes'=8,'cheb'=4] {'modes','cheb'}, use_global_device_ids=true, to_apply=%region_24.25 | all-reduce | flops 4 | bytes 32 | tf_op jit(solution)/shard_map/psum | solution.py:178
  859.6 19.1 %all_to_all.298 = f32[32,1,4096]{2,1,0:T(1,128)S(1)} all-to-all(f32[32,1,4096]{2,1,0:T(1,128)S(1)} %reshape.360), channel_id=1, replica_groups=mesh['modes'=8,'cheb'=4] {'modes','cheb'}, dimensions={0} | all-to-all | bytes 1048576 | tf_op jit(solution)/shard_map/all_to_all | solution.py:140
  908.6 7.2 reshape.362
  915.8 13.5 %all_to_all.299 = f32[32,1,2048]{2,1,0:T(1,128)S(1)} all-to-all(f32[32,1,2048]{2,1,0:T(1,128)S(1)} %reshape.362), channel_id=1, replica_groups=mesh['modes'=8,'cheb'=4] {'modes','cheb'}, dimensions={0} | all-to-all | bytes 524288 | tf_op jit(solution)/shard_map/all_to_all | solution.py:143
  930.6 7.6 reshape.363
  944.4 17.4 %fusion.2 = f32[64,2,2,256]{3,2,1,0:T(2,128)S(1)} fusion(f32[64,256,256]{2,1,0:T(8,128)} %param.5, f32[2,2,64,256]{3,2,1,0:T(8,128)S(1)} %fusion.80), kind=kOutput, calls=%fused_computation.2 | convolution fusion | flops 201326592 | bytes 17301504 | tf_op jit(solution)/shard_map/kam,brkm->brka/dot_general | solution.py:158
  962.0 38.6 %all-reduce.1 = (f32[2]{0:T(128)S(1)}, f32[2,2]{0,1:T(2,128)S(1)}) all-reduce(f32[2]{0:T(128)S(1)} %get-tuple-element.10, f32[2,2]{0,1:T(2,128)S(1)} %pad_maximum_fusion.11), channel_id=1, replica_groups=mesh['modes'=8,'cheb'=4] {'modes','cheb'}, use_global_device_ids=true, to_apply=%region_29.30 | all-reduce | flops 6 | bytes 48 | tf_op jit(solution)/shard_map/psum | solution.py:178
  1006.7 19.3 %all_to_all.300 = f32[32,1,4096]{2,1,0:T(1,128)S(1)} all-to-all(f32[32,1,4096]{2,1,0:T(1,128)} %reshape.364), channel_id=1, replica_groups=mesh['modes'=8,'cheb'=4] {'modes','cheb'}, dimensions={0} | all-to-all | bytes 1048576 | tf_op jit(solution)/shard_map/all_to_all | solution.py:140
  1058.0 7.3 reshape.366
  1065.2 13.5 %all_to_all.301 = f32[32,1,2048]{2,1,0:T(1,128)S(1)} all-to-all(f32[32,1,2048]{2,1,0:T(1,128)S(1)} %reshape.366), channel_id=1, replica_groups=mesh['modes'=8,'cheb'=4] {'modes','cheb'}, dimensions={0} | all-to-all | bytes 524288 | tf_op jit(solution)/shard_map/all_to_all | solution.py:143
  1080.0 7.6 reshape.367
  1093.8 17.4 %fusion = f32[64,2,2,256]{3,2,1,0:T(2,128)S(1)} fusion(f32[64,256,256]{2,1,0:T(8,128)} %param.5, f32[2,2,64,256]{3,2,1,0:T(8,128)S(1)} %fusion.81), kind=kOutput, calls=%fused_computation | convolution fusion | flops 201326592 | bytes 17301504 | tf_op jit(solution)/shard_map/kam,brkm->brka/dot_general | solution.py:158
  1111.4 38.6 %all-reduce = (f32[2]{0:T(128)S(1)}, f32[2,3]{0,1:T(4,128)S(1)}) all-reduce(f32[2]{0:T(128)S(1)} %get-tuple-element.7, f32[2,3]{0,1:T(4,128)S(1)} %pad_maximum_fusion.9), channel_id=1, replica_groups=mesh['modes'=8,'cheb'=4] {'modes','cheb'}, use_global_device_ids=true, to_apply=%region_36.37 | all-reduce | flops 8 | bytes 64 | tf_op jit(solution)/shard_map/psum | solution.py:178
  (332 shorter events, 327.0 us)
Async XLA Ops:
  5.2 23.0 %all-to-all-start = ((f32[32,1,4096]{2,1,0:T(1,128)}), f32[32,1,4096]{2,1,0:T(1,128)S(1)}, u32[]{:S(2)}, u32[]{:S(2)}) async-start(f32[32,1,4096]{2,1,0:T(1,128)} %reshape.336), calls=%async_computation | async-start | bytes 1048576 | tf_op jit(solution)/shard_map/all_to_all | solution.py:140
  42.3 45.0 %copy-start.5 = (f32[2,2,64,256]{3,2,1,0:T(8,128)S(1)}, f32[2,2,64,256]{3,2,1,0:T(8,128)}, u32[]{:S(2)}) copy-start(f32[2,2,64,256]{3,2,1,0:T(8,128)} %param.4) | copy-start | bytes 786436
  52.4 54.0 %copy-start = (f32[2,2,64,256]{3,2,1,0:T(8,128)S(1)}, f32[2,2,64,256]{3,2,1,0:T(8,128)}, u32[]{:S(2)}) copy-start(f32[2,2,64,256]{3,2,1,0:T(8,128)} %param.3) | copy-start | bytes 786436
  60.3 13.7 %all-to-all-start.1 = ((f32[32,1,2048]{2,1,0:T(1,128)}), f32[32,1,2048]{2,1,0:T(1,128)S(1)}, u32[]{:S(2)}, u32[]{:S(2)}) async-start(f32[32,1,2048]{2,1,0:T(1,128)} %reshape.338), calls=%async_computation.1 | async-start | bytes 524288 | tf_op jit(solution)/shard_map/all_to_all | solution.py:143
  431.1 104.0 %copy-start.4 = (f32[2,2,64,256]{3,2,1,0:T(8,128)}, f32[2,2,64,256]{3,2,1,0:T(8,128)S(1)}, u32[]{:S(2)}) copy-start(f32[2,2,64,256]{3,2,1,0:T(8,128)S(1)} %subtract_divide_fusion.2) | copy-start | bytes 786436
  481.9 92.2 %copy-start.1 = (f32[2,2,64,256]{3,2,1,0:T(8,128)S(1)}, f32[2,2,64,256]{3,2,1,0:T(8,128)}, u32[]{:S(2)}) copy-start(f32[2,2,64,256]{3,2,1,0:T(8,128)} %param.3) | copy-start | bytes 786436
  611.3 44.1 %copy-start.6 = (f32[2,2,64,256]{3,2,1,0:T(8,128)S(1)}, f32[2,2,64,256]{3,2,1,0:T(8,128)}, u32[]{:S(2)}) copy-start(f32[2,2,64,256]{3,2,1,0:T(8,128)} %param.4) | copy-start | bytes 786436
  1000.8 38.3 %copy-start.2 = (f32[2,2,64,256]{3,2,1,0:T(8,128)}, f32[2,2,64,256]{3,2,1,0:T(8,128)S(1)}, u32[]{:S(2)}) copy-start(f32[2,2,64,256]{3,2,1,0:T(8,128)S(1)} %subtract_divide_fusion) | copy-start | bytes 786436
  1058.0 53.2 %copy-start.3 = (f32[2,2,64,256]{3,2,1,0:T(8,128)S(1)}, f32[2,2,64,256]{3,2,1,0:T(8,128)}, u32[]{:S(2)}) copy-start(f32[2,2,64,256]{3,2,1,0:T(8,128)} %copy-done.2) | copy-start | bytes 786436
where the time goes:
time: 1160 us; the launch traced here: 1150 us
  blocking collectives  537 us (46%)
  matrix products  312 us (27%)
  local copies, waits for them, and re-layouts  229 us (20%)
  other arithmetic  34.4 us (3%)
  waiting for transfers between devices  25.4 us (2%)
    psum x6, blocking collectives, shards(): lax.psum((local_dots, local_square), ('modes', 'cheb'))  232 us
    dot_general x8, matrix products, precondition(): return jnp.einsum('kam,brkm->brka', taus, coefs * tau_keep, precision=HIGH)  139 us
    unnamed x46, local copies, waits for them, and re-layouts  137 us
    all_to_all x7, blocking collectives, move_out(): lax.all_to_all(stacked, ('modes', 'cheb'), split_axis=3, concat_axis=4, t...  134 us
    all_to_all x7, blocking collectives, move_back(): lax.all_to_all(spectrum, ('modes', 'cheb'), split_axis=3, concat_axis=2,...  94.6 us
    psum x2, blocking collectives, shards(): lax.psum(jnp.sum(residual * residual, axis=(1, 2, 3)), ('modes', 'cheb'))  77.1 us
    all_to_all x8, local copies, waits for them, and re-layouts, move_back(): lax.all_to_all(spectrum, ('modes', 'cheb'), split_axis=3, concat_axis=2,...  35.3 us
    mul x8, local copies, waits for them, and re-layouts, forward_modes(): return jnp.stack([coef_real, coef_imag], axis=-3) * factor  34.5 us
  transfers between devices with their start and end apart: 2, of which 2 were waited for; matrix products, arithmetic and copies ran while one was open for 0% of the time, Pallas kernels for 0%

commit v1 on v0

v1 whole, which is shorter than its diff:
```python
import math

import jax
import jax.numpy as jnp
import numpy as np
from jax import lax
from jax.experimental import pallas as pl
from jax.experimental.pallas import tpu as pltpu
from jax.sharding import PartitionSpec as P

NEWTON = 2
KRYLOV = 3
STRENGTH = 0.1
AXES = ("modes", "cheb")
F32 = jnp.float32
BF16 = jnp.bfloat16
DOTS = 8


def halves(table):
    table = np.asarray(table, np.float32)
    high = table.astype(BF16)
    low = (table - high.astype(np.float32)).astype(BF16)
    return np.stack([high, low])


def split(x):
    high = x.astype(BF16)
    return high, (x - high.astype(F32)).astype(BF16)


def mm(a, b):
    return lax.dot_general(a, b, (((1,), (0,)), ((), ())), preferred_element_type=F32)


def table_left(t_ref, x):
    high, low = split(x)
    return mm(t_ref[0], high) + (mm(t_ref[0], low) + mm(t_ref[1], high))


def table_right(x, t_ref):
    high, low = split(x)
    return mm(high, t_ref[0]) + (mm(low, t_ref[0]) + mm(high, t_ref[1]))


def least_squares(hessen, beta_norm):
    steps_count = len(hessen)
    matrix = [list(column) for column in hessen]
    target = [beta_norm] + [jnp.zeros_like(beta_norm)] * steps_count
    cosines = []
    sines = []
    for col in range(steps_count):
        column = matrix[col]
        for row in range(col):
            upper = cosines[row] * column[row] + sines[row] * column[row + 1]
            lower = cosines[row] * column[row + 1] - sines[row] * column[row]
            column[row] = upper
            column[row + 1] = lower
        radius = jnp.sqrt(column[col] * column[col] + column[col + 1] * column[col + 1])
        cosines.append(column[col] / radius)
        sines.append(column[col + 1] / radius)
        column[col] = radius
        target[col + 1] = -sines[col] * target[col]
        target[col] = cosines[col] * target[col]
    solved = [None] * steps_count
    for row in reversed(range(steps_count)):
        partial = target[row]
        for col in range(row + 1, steps_count):
            partial = partial - matrix[col][row] * solved[col]
        solved[row] = partial / matrix[row][row]
    return solved


class Plan:
    def __init__(self, group, batch, kl, ny):
        self.group, self.batch, self.kl, self.ny = group, batch, kl, ny
        self.il = ny // group
        self.bq = batch * kl
        self.j1 = 2 * group
        self.direct = self.il % 8 == 0 and self.bq % 128 == 0
        modes = kl * group
        points = 2 * modes
        spread = 1.0 / math.sqrt(modes * ny)
        tau = 2.0 * np.pi
        n, i = np.arange(ny)[:, None], np.arange(ny)[None, :]
        cheb = np.cos(tau / (4 * ny) * (n * (2 * i + 1) % (4 * ny)))
        self.ct = halves(cheb.T)
        self.cw = halves(cheb * (np.where(n == 0, 1.0, 2.0) / ny))
        d, j = np.arange(group)[None, :], np.arange(self.j1)[:, None]
        angle = tau / self.j1 * (d * j % self.j1)
        co, si = np.cos(angle), np.sin(angle)
        slope = 16.0 / modes * kl * d
        self.t1 = halves(np.block([
            [co, -si], [si, co], [-slope * si, -slope * co], [slope * co, -slope * si],
        ]))
        scale = STRENGTH / (spread * points)
        self.t4 = halves(scale * np.block([[co.T, si.T], [-si.T, co.T]]))
        q = np.arange(kl)
        twist = tau / points * (j * q[None, :] % points)
        slope_q = np.broadcast_to(16.0 / modes * q[None, :], twist.shape)
        self.tw = np.stack([
            np.tile(t, (1, batch)) for t in (np.cos(twist), np.sin(twist), slope_q)
        ]).astype(np.float32)
        weight = np.full((group, kl), 2.0 * spread)
        weight[0, 0] = spread
        self.wt = np.tile(weight, (2, batch)).astype(np.float32)
        inner = tau / kl * (q[:, None] * q[None, :] % kl)
        eye = np.eye(batch)
        self.b2 = halves(np.concatenate([np.kron(eye, np.cos(inner)), np.kron(eye, -np.sin(inner))], 0))
        self.b3 = halves(np.concatenate([np.kron(eye, np.cos(inner)), np.kron(eye, -np.sin(inner))], 1))
        self.ones = np.kron(eye, np.ones((kl, kl))).astype(np.float32)

    def tables(self):
        return [self.t1, self.tw, self.wt, self.b2, self.b3, self.t4, self.ones]


def flow_sums(dots, ones_ref):
    total = jnp.sum(dots, axis=0)
    return jnp.dot(total, ones_ref[...], precision=lax.Precision.HIGHEST, preferred_element_type=F32)


def new_column(sums, count):
    heads = [sums[i : i + 1] for i in range(count)]
    square = sums[count : count + 1]
    for head in heads:
        square = square - head * head
    return heads + [jnp.sqrt(square)]


def solve_rows(sums, scal):
    hessen = [[s[i : i + 1] for i in range(n + 2)] for n, s in enumerate(scal[1:])]
    hessen.append(new_column(sums, KRYLOV))
    return least_squares(hessen, scal[0][0:1])


def put_rows(ref, rows):
    ref[...] = jnp.zeros(ref.shape, F32)
    for index, row in enumerate(rows):
        ref[index : index + 1, :] = row


def points_call(plan, mode, field=None, dots=None, base=None, basis=(), scal=()):
    group, il, bq, j1 = plan.group, plan.il, plan.bq, plan.j1
    stride_in, stride_out = 2 * il + DOTS, 2 * il
    names, args = [], []

    def add(name, value):
        names.append(name)
        args.append(value)

    for name, value in zip(("t1", "tw", "wt", "b2", "b3", "t4", "ones"), plan.tables()):
        add(name, jnp.asarray(value))
    if field is not None:
        add("field", field)
    if dots is not None:
        add("dots", dots)
    if base is not None:
        add("base", base)
    for i, v in enumerate(basis):
        add(f"v{i}", v)
    for i, v in enumerate(scal):
        add(f"s{i}", v)
    pts_shape = jax.ShapeDtypeStruct((il, 2, j1, bq), F32)
    if plan.direct:
        send_shape = jax.ShapeDtypeStruct((group * stride_out, bq), F32)
    else:
        send_shape = jax.ShapeDtypeStruct((2 * group, il * bq), F32)
    outs = [send_shape, pts_shape]
    if mode != "start":
        outs.append(jax.ShapeDtypeStruct((DOTS, bq), F32))

    def kernel(*refs):
        ins = dict(zip(names, refs[: len(names)]))
        send, pts_out = refs[len(names)], refs[len(names) + 1]
        rows_out = refs[len(names) + 2] if mode != "start" else None

        def to_points():
            if plan.direct:
                sides = [
                    jnp.concatenate(
                        [ins["field"][pl.ds(r * il + i, group, stride=stride_in), :] for i in range(il)],
                        axis=1,
                    )
                    for r in range(2)
                ]
                x = jnp.concatenate(sides, axis=0)
            else:
                x = ins["field"][...]
            x = x * jnp.concatenate([ins["wt"][...]] * il, axis=1)
            z = table_left(ins["t1"], x)
            co, si, gq = ins["tw"][0], ins["tw"][1], ins["tw"][2]
            rows = []
            for i in range(il):
                part = z[:, i * bq : (i + 1) * bq]
                re, im = part[:j1], part[j1 : 2 * j1]
                sre = part[2 * j1 : 3 * j1] - gq * im
                sim = part[3 * j1 :] + gq * re
                for a, b in ((re, im), (sre, sim)):
                    rows.append(jnp.concatenate([a * co - b * si, a * si + b * co], axis=1))
            return table_right(jnp.concatenate(rows, axis=0), ins["b2"]).reshape(il, 2, j1, bq)

        if mode == "start":
            pts = to_points()
            pts_out[...] = pts
            product = pts[:, 0] * pts[:, 1]
        elif mode == "basis":
            if plan.direct:
                parts = ins["field"][...].reshape(group, stride_in, bq)[:, 2 * il :, :]
            else:
                parts = ins["dots"][...]
            sums = flow_sums(parts, ins["ones"])
            pts = to_points()
            if not basis:
                column = [jnp.sqrt(sums[0:1])]
                pts = pts * (-1.0 / column[0])
            else:
                column = new_column(sums, len(basis))
                for i in range(len(basis)):
                    pts = pts - column[i] * ins[f"v{i}"][...]
                pts = pts * (1.0 / column[-1])
            put_rows(rows_out, column)
            pts_out[...] = pts
            product = ins["base"][:, 0] * pts[:, 1] + pts[:, 0] * ins["base"][:, 1]
        else:
            sums = flow_sums(ins["dots"][...], ins["ones"])
            solved = solve_rows(sums, [ins[f"s{i}"][...] for i in range(KRYLOV)])
            pts = ins["base"][...]
            for i in range(KRYLOV):
                pts = pts + solved[i] * ins[f"v{i}"][...]
            put_rows(rows_out, solved)
            pts_out[...] = pts
            product = pts[:, 0] * pts[:, 1]
        part = table_right(product.reshape(il * j1, bq), ins["b3"])
        co, si = ins["tw"][0], ins["tw"][1]
        cols = []
        for i in range(il):
            re, im = part[i * j1 : (i + 1) * j1, :bq], part[i * j1 : (i + 1) * j1, bq:]
            cols.append(jnp.concatenate([re * co + im * si, im * co - re * si], axis=0))
        out = table_left(ins["t4"], jnp.concatenate(cols, axis=1))
        if plan.direct:
            for r in range(2):
                for i in range(il):
                    send[pl.ds(r * il + i, group, stride=stride_out), :] = out[
                        r * group : (r + 1) * group, i * bq : (i + 1) * bq
                    ]
        else:
            send[...] = out

    return pl.pallas_call(kernel, out_shape=outs, name=f"points_{mode}_{len(basis)}")(*args)


def spectral_call(plan, mode, recv, taus, states, basis=(), scal=None, emit=True):
    group, il, bq, ny, kl = plan.group, plan.il, plan.bq, plan.ny, plan.kl
    wide = 2 * bq
    qb = min(8, kl)
    steps = kl // qb
    lines = wide
    names, args, specs = [], [], []

    def add(name, value):
        names.append(name)
        args.append(value)
        rank = value.ndim
        specs.append(pl.BlockSpec(value.shape, lambda s, rank=rank: (0,) * rank))

    add("recv", recv)
    add("ct", jnp.asarray(plan.ct))
    add("cw", jnp.asarray(plan.cw))
    for i, v in enumerate(states):
        add(f"x{i}", v)
    for i, v in enumerate(basis):
        add(f"v{i}", v)
    if scal is not None:
        add("scal", scal)
    names.append("taus")
    args.append(taus)
    specs.append(pl.BlockSpec((qb, ny, ny), lambda s: (s, 0, 0)))

    state_shape = jax.ShapeDtypeStruct((ny, wide), F32)
    out_names, outs = [], []
    if mode == "residual":
        if basis:
            out_names.append("iterate")
            outs.append(state_shape)
    else:
        out_names.append("vector")
        outs.append(state_shape)
    if emit:
        out_names.append("applied")
        outs.append(state_shape)
        out_names.append("send")
        if plan.direct:
            outs.append(jax.ShapeDtypeStruct((group, 2 * il + DOTS, bq), F32))
        else:
            outs.append(jax.ShapeDtypeStruct((2, ny, bq), F32))
    if not (emit and plan.direct):
        out_names.append("dots")
        outs.append(jax.ShapeDtypeStruct((DOTS, bq), F32))
    out_specs = [
        pl.BlockSpec(o.shape, lambda s, rank=len(o.shape): (0,) * rank) for o in outs
    ]

    def kernel(*refs):
        ins = dict(zip(names, refs[: len(names)]))
        res = dict(zip(out_names, refs[len(names) : len(names) + len(outs)]))
        c_scr, m_scr = refs[len(names) + len(outs) :]
        step = pl.program_id(0)

        @pl.when(step == 0)
        def _():
            if plan.direct:
                sides = [
                    ins["recv"][:, r * il : (r + 1) * il, :].reshape(ny, bq) for r in range(2)
                ]
            else:
                sides = [ins["recv"][r] for r in range(2)]
            coef = table_left(ins["cw"], jnp.concatenate(sides, axis=1))
            if mode == "residual":
                coef = coef - ins["x1"][...]
            degree = lax.broadcasted_iota(jnp.int32, coef.shape, 0)
            coef = jnp.where(degree < ny - 2, coef, 0.0).T
            high = coef.astype(BF16).astype(F32)
            for h in range(ny // 128):
                c_scr[h, :lines, :] = high[:, h * 128 : (h + 1) * 128]
                c_scr[h, lines:, :] = (coef - high)[:, h * 128 : (h + 1) * 128]

        for t in range(qb):
            q = step * qb + t
            picked = pl.ds(q, 2 * lines // kl, stride=kl)
            rows = jnp.concatenate([c_scr[h, picked, :] for h in range(ny // 128)], axis=1).astype(BF16)
            high, low = split(ins["taus"][t])
            dims = (((1,), (1,)), ((), ()))
            got = lax.dot_general(rows, high, dims, preferred_element_type=F32)
            got = got + lax.dot_general(rows, low, dims, preferred_element_type=F32)
            for h in range(ny // 128):
                m_scr[h, picked, :] = got[:, h * 128 : (h + 1) * 128]

        @pl.when(step == steps - 1)
        def _():
            mapped = jnp.concatenate(
                [m_scr[h, :lines, :] + m_scr[h, lines:, :] for h in range(ny // 128)], axis=1
            ).T

            def row(index):
                r = ins["scal"][index : index + 1, :]
                return jnp.concatenate([r, r], axis=1)

            vector = ins["x0"][...]
            if mode == "residual":
                if basis:
                    for i in range(len(basis)):
                        vector = vector + row(i) * ins[f"v{i}"][...]
                    res["iterate"][...] = vector
                others = []
            else:
                if not basis:
                    vector = vector * (-1.0 / row(0))
                else:
                    for i in range(len(basis)):
                        vector = vector - row(i) * ins[f"v{i}"][...]
                    vector = vector * (1.0 / row(len(basis)))
                res["vector"][...] = vector
                others = [ins[f"v{i}"][...] for i in range(len(basis))] + [vector]
            applied = vector + mapped
            lanes = []
            for other in others + [applied]:
                dot = jnp.sum(other * applied, axis=0, keepdims=True)
                lanes.append(dot[:, :bq] + dot[:, bq:])
            lanes += [jnp.zeros((1, bq), F32)] * (DOTS - len(lanes))
            dots = jnp.concatenate(lanes, axis=0)
            if emit:
                res["applied"][...] = applied
                values = table_left(ins["ct"], applied)
                for r in range(2):
                    side = values[:, r * bq : (r + 1) * bq]
                    if plan.direct:
                        res["send"][:, r * il : (r + 1) * il, :] = side.reshape(group, il, bq)
                    else:
                        res["send"][r] = side
            if emit and plan.direct:
                res["send"][:, 2 * il :, :] = jnp.broadcast_to(dots[None], (group, DOTS, bq))
            else:
                res["dots"][...] = dots

    got = pl.pallas_call(
        kernel,
        grid=(steps,),
        in_specs=specs,
        out_specs=out_specs,
        out_shape=outs,
        scratch_shapes=[pltpu.VMEM((ny // 128, 2 * lines, 128), F32)] * 2,
        compiler_params=pltpu.CompilerParams(dimension_semantics=("arbitrary",)),
        name=f"spectral_{mode}_{len(basis)}",
    )(*args)
    return dict(zip(out_names, got))


def finish_call(plan, dots, iterate, basis, scal):
    ones = jnp.asarray(plan.ones)

    def kernel(*refs):
        out = refs[-1]
        sums = flow_sums(refs[0][...], refs[1])
        solved = solve_rows(sums, [r[...] for r in refs[3 + KRYLOV : 3 + 2 * KRYLOV]])
        value = refs[2][...]
        for i in range(KRYLOV):
            value = value + jnp.concatenate([solved[i]] * 2, axis=1) * refs[3 + i][...]
        out[...] = value

    shape = jax.ShapeDtypeStruct(iterate.shape, F32)
    return pl.pallas_call(kernel, out_shape=shape, name="finish")(dots, ones, iterate, *basis, *scal)


def values_call(plan, state):
    group, il, bq, ny = plan.group, plan.il, plan.bq, plan.ny
    if plan.direct:
        shape = jax.ShapeDtypeStruct((group, 2 * il + DOTS, bq), F32)
    else:
        shape = jax.ShapeDtypeStruct((2, ny, bq), F32)

    def kernel(ct, x, send):
        values = table_left(ct, x[...])
        for r in range(2):
            side = values[:, r * bq : (r + 1) * bq]
            if plan.direct:
                send[:, r * il : (r + 1) * il, :] = side.reshape(group, il, bq)
            else:
                send[r] = side
        if plan.direct:
            send[:, 2 * il :, :] = jnp.zeros((group, DOTS, bq), F32)

    return pl.pallas_call(kernel, out_shape=shape, name="values")(jnp.asarray(plan.ct), state)


def shards(start, forcing, taus):
    batch, _, kl, ny = start.shape
    group = lax.axis_size(AXES)
    plan = Plan(group, batch, kl, ny)
    il, bq = plan.il, plan.bq

    def swap(x):
        return lax.all_to_all(x, AXES, split_axis=0, concat_axis=0, tiled=True)

    def gather_dots(dots):
        return swap(jnp.broadcast_to(dots[None], (group,) + dots.shape))

    def move_out(sent, dots=None):
        if plan.direct:
            got = swap(sent)
            return got.reshape(group * (2 * il + DOTS), bq), None
        blocks = sent.reshape(2, group, il, bq).transpose(1, 0, 2, 3).reshape(group, 2 * il, bq)
        got = swap(blocks).reshape(group, 2, il, bq).transpose(1, 0, 2, 3)
        return got.reshape(2 * group, il * bq), None if dots is None else gather_dots(dots)

    def move_back(sent):
        if plan.direct:
            return swap(sent.reshape(group, 2 * il, bq))
        blocks = sent.reshape(2, group, il, bq).transpose(1, 0, 2, 3).reshape(group, 2 * il, bq)
        return swap(blocks).reshape(group, 2, il, bq).transpose(1, 0, 2, 3).reshape(2, ny, bq)

    def to_state(x):
        return x.transpose(3, 1, 0, 2).reshape(ny, 2 * bq)

    iterate, forced = to_state(start), to_state(forcing)
    field, _ = move_out(values_call(plan, iterate))
    sent, base = points_call(plan, "start", field)
    basis, solved = [], None
    for newton_step in range(NEWTON):
        got = spectral_call(plan, "residual", move_back(sent), taus, (iterate, forced), basis, solved)
        iterate = got.get("iterate", iterate)
        basis, basis_pts, scal = [], [], []
        for column in range(KRYLOV):
            field, dots = move_out(got["send"], got.get("dots"))
            sent, pts, rows = points_call(plan, "basis", field, dots, base, basis_pts)
            scal.append(rows)
            basis_pts.append(pts)
            got = spectral_call(
                plan, "krylov", move_back(sent), taus, (got["applied"],), basis, rows,
                emit=column < KRYLOV - 1,
            )
            basis.append(got["vector"])
        dots = gather_dots(got["dots"])
        if newton_step < NEWTON - 1:
            sent, base, solved = points_call(plan, "restart", None, dots, base, basis_pts, scal)
        else:
            iterate = finish_call(plan, dots, iterate, basis, scal)
    return iterate.reshape(ny, 2, batch, kl).transpose(2, 1, 3, 0)


def solution(mesh):
    return jax.shard_map(
        shards,
        mesh=mesh,
        in_specs=(
            P(None, None, AXES, None),
            P(None, None, AXES, None),
            P(AXES, None, None),
        ),
        out_specs=P(None, None, AXES, None),
        check_vma=False,
    )
```

time: 1160 us -> 396 us (0.34)
  matrix products: 312 us -> 0 us
  blocking collectives: 537 us -> 238 us
  local copies, waits for them, and re-layouts: 229 us -> 7.48 us
  Pallas kernels: 0 us -> 137 us
  other arithmetic: 34.4 us -> 0 us
  waiting for transfers between devices: 25.4 us -> 8.77 us
    dot_general x120 -> x0, matrix products: 312 us -> none  [the longest x8 139 us: precondition(): return jnp.einsum('kam,brkm->brka', taus, coefs * tau_keep, precision=HIGH)]
    psum x8 -> x0, blocking collectives: 309 us -> none  [the longest x6 232 us: shards(): lax.psum((local_dots, local_square), ('modes', 'cheb'))]
    pallas_call x0 -> x18, Pallas kernels: none -> 137 us  [the longest x8 97.7 us: spectral_call(): pl.pallas_call(kernel, grid=(steps,), in_specs=specs, out_specs=out_specs...]
    unnamed x46 -> x4, local copies, waits for them, and re-layouts: 137 us -> 2.64 us
    all_to_all x33 -> x0, local copies, waits for them, and re-layouts: 42.7 us -> none  [the longest x8 35.3 us: move_back(): lax.all_to_all(spectrum, ('modes', 'cheb'), split_axis=3, concat_axis=2,...]
    mul x8 -> x0, local copies, waits for them, and re-layouts: 34.5 us -> none  [forward_modes(): return jnp.stack([coef_real, coef_imag], axis=-3) * factor]
    all_to_all x16 -> x0, other arithmetic: 25.6 us -> none  [the longest x8 15.8 us: move_out(): lax.all_to_all(stacked, ('modes', 'cheb'), split_axis=3, concat_axis=4, t...]
    all_to_all x2 -> x1, waiting for transfers between devices: 25.4 us -> 8.77 us  [swap(): return lax.all_to_all(x, AXES, split_axis=0, concat_axis=0, tiled=True)]
  transfers between devices with their start and end apart: 2 -> 1, of which waited for: 2 -> 1; matrix products, arithmetic and copies ran while one was open for 0% -> 0% of each run, Pallas kernels for 0% -> 0%
where the time goes in v1:
time: 396 us; the launch traced here: 394 us
  blocking collectives  238 us (60%)
  Pallas kernels  137 us (35%)
  waiting for transfers between devices  8.77 us (2%)
  local copies, waits for them, and re-layouts  7.48 us (2%)
    all_to_all x16, blocking collectives, swap(): return lax.all_to_all(x, AXES, split_axis=0, concat_axis=0, tiled=True)  238 us
    pallas_call x8, Pallas kernels, spectral_call(): pl.pallas_call(kernel, grid=(steps,), in_specs=specs, out_specs=out_specs...  97.7 us
    pallas_call x8, Pallas kernels, points_call(): pl.pallas_call(kernel, out_shape=outs, name=f'points_{mode}_{len(basis)}')  34.7 us
    all_to_all x1, waiting for transfers between devices, swap(): return lax.all_to_all(x, AXES, split_axis=0, concat_axis=0, tiled=True)  8.77 us
  transfers between devices with their start and end apart: 1, of which 1 were waited for; matrix products, arithmetic and copies ran while one was open for 0% of the time, Pallas kernels for 0%

profile of v1, /device:TPU:0, one launch (start us, length us, event | category | flops | bytes accessed | tf_op | source)
XLA Modules:
  0.0 393.7 jit_solution(4303820391114822817)
XLA Ops:
  0.0 1.0 copy.16
  1.0 0.8 copy.17.x.refs_3_
  1.8 2.1 values.1
  3.9 20.7 %all_to_all.85 = f32[32,24,128]{2,1,0:T(8,128)} all-to-all(f32[32,24,128]{2,1,0:T(8,128)} %values.1), channel_id=1, replica_groups=mesh['modes'=8,'cheb'=4] {'modes','cheb'}, dimensions={0} | all-to-all | bytes 786432 | tf_op jit(solution)/shard_map/all_to_all | solution.py:442
  24.6 4.1 %points_start_0.1 = (f32[512,128]{1,0:T(8,128)}, f32[8,2,64,128]{3,2,1,0:T(8,128)}) custom-call(bf16[2,256,64]{2,1,0:T(8,128)(2,1)} %constant.19.clone.refs_0_, f32[3,64,128]{2,1,0:T(8,128)} %constant.20.clone.refs_1_, f32[64,128]{1,0:T(8,128)} %constant.21.clone.refs_2_, bf16[2,256,128]{2,1,0:T(8,128)(2,1)} %constant.22.clone.refs_3_, ...), custom_call_target="tpu_custom_call" | custom-call | tf_op jit(solution)/shard_map/points_start_0/pallas_call | solution.py:249
  28.6 2.6 all-to-all-start.1
  31.2 1.0 copy.18
  32.2 0.8 copy.20.refs_4_
  33.0 8.8 %all-to-all-done.1.refs_0_ = f32[32,16,128]{2,1,0:T(8,128)S(1)} async-done(((f32[32,16,128]{2,1,0:T(8,128)}), f32[32,16,128]{2,1,0:T(8,128)S(1)}, u32[]{:S(2)}, u32[]{:S(2)}) %all-to-all-start.1) | async-done | bytes 262176 | tf_op jit(solution)/shard_map/all_to_all | solution.py:442
  41.8 0.0 copy-start
  41.8 0.7 copy-done
  42.5 12.2 %spectral_residual_0.1 = (f32[256,256]{1,0:T(8,128)}, f32[32,24,128]{2,1,0:T(8,128)}) custom-call(f32[32,16,128]{2,1,0:T(8,128)} %copy-done, bf16[2,256,256]{2,1,0:T(8,128)(2,1)} %constant.18.clone.ct.refs_1_, bf16[2,256,256]{2,1,0:T(8,128)(2,1)} %constant.26.clone.refs_2_, f32[256,256]{1,0:T(8,128)} %copy.17.x.refs_3_, f32[256,256]{1,0:T(8,128)} %copy.20.refs_4_, ...), custom_call_target="tpu_custom_call" | custom-call | tf_op jit(solution)/shard_map/spectral_residual_0/pallas_call | solution.py:385
  54.7 16.5 %all_to_all.86 = f32[32,24,128]{2,1,0:T(8,128)} all-to-all(f32[32,24,128]{2,1,0:T(8,128)} %get-tuple-element.49), channel_id=1, replica_groups=mesh['modes'=8,'cheb'=4] {'modes','cheb'}, dimensions={0} | all-to-all | bytes 786432 | tf_op jit(solution)/shard_map/all_to_all | solution.py:442
  71.2 4.3 %points_basis_0.2 = (f32[512,128]{1,0:T(8,128)}, f32[8,2,64,128]{3,2,1,0:T(8,128)}, f32[8,128]{1,0:T(8,128)}) custom-call(bf16[2,256,64]{2,1,0:T(8,128)(2,1)} %constant.19.clone.refs_0_, f32[3,64,128]{2,1,0:T(8,128)} %constant.20.clone.refs_1_, f32[64,128]{1,0:T(8,128)} %constant.21.clone.refs_2_, bf16[2,256,128]{2,1,0:T(8,128)(2,1)} %constant.22.clone.refs_3_, ...), custom_call_target="tpu_custom_call" | custom-call | tf_op jit(solution)/shard_map/points_basis_0/pallas_call | solution.py:249
  75.6 13.9 %all_to_all.87.refs_0_ = f32[32,16,128]{2,1,0:T(8,128)} all-to-all(f32[32,16,128]{2,1,0:T(8,128)} %bitcast.37), channel_id=1, replica_groups=mesh['modes'=8,'cheb'=4] {'modes','cheb'}, dimensions={0} | all-to-all | bytes 524288 | tf_op jit(solution)/shard_map/all_to_all | solution.py:442
  89.4 12.2 %spectral_krylov_0.2 = (f32[256,256]{1,0:T(8,128)}, f32[256,256]{1,0:T(8,128)}, f32[32,24,128]{2,1,0:T(8,128)}) custom-call(f32[32,16,128]{2,1,0:T(8,128)} %all_to_all.87.refs_0_, bf16[2,256,256]{2,1,0:T(8,128)(2,1)} %constant.18.clone.ct.refs_1_, bf16[2,256,256]{2,1,0:T(8,128)(2,1)} %constant.26.clone.refs_2_, f32[256,256]{1,0:T(8,128)} %get-tuple-element.52.refs_3_, ...), custom_call_target="tpu_custom_call" | custom-call | tf_op jit(solution)/shard_map/spectral_krylov_0/pallas_call | solution.py:385
  101.6 16.5 %all_to_all.88 = f32[32,24,128]{2,1,0:T(8,128)} all-to-all(f32[32,24,128]{2,1,0:T(8,128)} %get-tuple-element.54), channel_id=1, replica_groups=mesh['modes'=8,'cheb'=4] {'modes','cheb'}, dimensions={0} | all-to-all | bytes 786432 | tf_op jit(solution)/shard_map/all_to_all | solution.py:442
  118.2 4.5 %points_basis_1.2 = (f32[512,128]{1,0:T(8,128)}, f32[8,2,64,128]{3,2,1,0:T(8,128)}, f32[8,128]{1,0:T(8,128)}) custom-call(bf16[2,256,64]{2,1,0:T(8,128)(2,1)} %constant.19.clone.refs_0_, f32[3,64,128]{2,1,0:T(8,128)} %constant.20.clone.refs_1_, f32[64,128]{1,0:T(8,128)} %constant.21.clone.refs_2_, bf16[2,256,128]{2,1,0:T(8,128)(2,1)} %constant.22.clone.refs_3_, ...), custom_call_target="tpu_custom_call" | custom-call | tf_op jit(solution)/shard_map/points_basis_1/pallas_call | solution.py:249
  122.7 13.9 %all_to_all.89.refs_0_ = f32[32,16,128]{2,1,0:T(8,128)} all-to-all(f32[32,16,128]{2,1,0:T(8,128)} %bitcast.38), channel_id=1, replica_groups=mesh['modes'=8,'cheb'=4] {'modes','cheb'}, dimensions={0} | all-to-all | bytes 524288 | tf_op jit(solution)/shard_map/all_to_all | solution.py:442
  136.5 12.3 %spectral_krylov_1.2 = (f32[256,256]{1,0:T(8,128)}, f32[256,256]{1,0:T(8,128)}, f32[32,24,128]{2,1,0:T(8,128)}) custom-call(f32[32,16,128]{2,1,0:T(8,128)} %all_to_all.89.refs_0_, bf16[2,256,256]{2,1,0:T(8,128)(2,1)} %constant.18.clone.ct.refs_1_, bf16[2,256,256]{2,1,0:T(8,128)(2,1)} %constant.26.clone.refs_2_, f32[256,256]{1,0:T(8,128)} %get-tuple-element.57.refs_3_, ...), custom_call_target="tpu_custom_call" | custom-call | tf_op jit(solution)/shard_map/spectral_krylov_1/pallas_call | solution.py:385
  148.8 16.5 %all_to_all.90 = f32[32,24,128]{2,1,0:T(8,128)} all-to-all(f32[32,24,128]{2,1,0:T(8,128)} %get-tuple-element.60), channel_id=1, replica_groups=mesh['modes'=8,'cheb'=4] {'modes','cheb'}, dimensions={0} | all-to-all | bytes 786432 | tf_op jit(solution)/shard_map/all_to_all | solution.py:442
  165.4 4.6 %points_basis_2.2 = (f32[512,128]{1,0:T(8,128)}, f32[8,2,64,128]{3,2,1,0:T(8,128)}, f32[8,128]{1,0:T(8,128)}) custom-call(bf16[2,256,64]{2,1,0:T(8,128)(2,1)} %constant.19.clone.refs_0_, f32[3,64,128]{2,1,0:T(8,128)} %constant.20.clone.refs_1_, f32[64,128]{1,0:T(8,128)} %constant.21.clone.refs_2_, bf16[2,256,128]{2,1,0:T(8,128)(2,1)} %constant.22.clone.refs_3_, ...), custom_call_target="tpu_custom_call" | custom-call | tf_op jit(solution)/shard_map/points_basis_2/pallas_call | solution.py:249
  170.0 13.9 %all_to_all.91.refs_0_ = f32[32,16,128]{2,1,0:T(8,128)} all-to-all(f32[32,16,128]{2,1,0:T(8,128)} %bitcast.39), channel_id=1, replica_groups=mesh['modes'=8,'cheb'=4] {'modes','cheb'}, dimensions={0} | all-to-all | bytes 524288 | tf_op jit(solution)/shard_map/all_to_all | solution.py:442
  183.9 11.9 %spectral_krylov_2.2 = (f32[256,256]{1,0:T(8,128)}, f32[8,128]{1,0:T(8,128)}) custom-call(f32[32,16,128]{2,1,0:T(8,128)} %all_to_all.91.refs_0_, bf16[2,256,256]{2,1,0:T(8,128)(2,1)} %constant.18.clone.ct.refs_1_, bf16[2,256,256]{2,1,0:T(8,128)(2,1)} %constant.26.clone.refs_2_, f32[256,256]{1,0:T(8,128)} %get-tuple-element.63.refs_3_, ...), custom_call_target="tpu_custom_call" | custom-call | tf_op jit(solution)/shard_map/spectral_krylov_2/pallas_call | solution.py:385
  195.8 0.7 broadcast_in_dim.4
  196.5 10.6 %all_to_all.92.refs_7_ = f32[32,8,128]{2,1,0:T(8,128)} all-to-all(f32[32,8,128]{2,1,0:T(8,128)S(1)} %broadcast_in_dim.4), channel_id=1, replica_groups=mesh['modes'=8,'cheb'=4] {'modes','cheb'}, dimensions={0} | all-to-all | bytes 262144 | tf_op jit(solution)/shard_map/all_to_all | solution.py:442
  207.1 3.7 points_restart_3.1
  210.7 13.9 %all_to_all.93.refs_0_ = f32[32,16,128]{2,1,0:T(8,128)} all-to-all(f32[32,16,128]{2,1,0:T(8,128)} %bitcast.35), channel_id=1, replica_groups=mesh['modes'=8,'cheb'=4] {'modes','cheb'}, dimensions={0} | all-to-all | bytes 524288 | tf_op jit(solution)/shard_map/all_to_all | solution.py:442
  224.6 12.6 %spectral_residual_3.1 = (f32[256,256]{1,0:T(8,128)}, f32[256,256]{1,0:T(8,128)}, f32[32,24,128]{2,1,0:T(8,128)}) custom-call(f32[32,16,128]{2,1,0:T(8,128)} %all_to_all.93.refs_0_, bf16[2,256,256]{2,1,0:T(8,128)(2,1)} %constant.18.clone.ct.refs_1_, bf16[2,256,256]{2,1,0:T(8,128)(2,1)} %constant.26.clone.refs_2_, f32[256,256]{1,0:T(8,128)} %copy.17.x.refs_3_, ...), custom_call_target="tpu_custom_call" | custom-call | tf_op jit(solution)/shard_map/spectral_residual_3/pallas_call | solution.py:385
  237.1 16.5 %all_to_all.94 = f32[32,24,128]{2,1,0:T(8,128)} all-to-all(f32[32,24,128]{2,1,0:T(8,128)} %get-tuple-element.71), channel_id=1, replica_groups=mesh['modes'=8,'cheb'=4] {'modes','cheb'}, dimensions={0} | all-to-all | bytes 786432 | tf_op jit(solution)/shard_map/all_to_all | solution.py:442
  253.7 4.3 %points_basis_0.3 = (f32[512,128]{1,0:T(8,128)}, f32[8,2,64,128]{3,2,1,0:T(8,128)}, f32[8,128]{1,0:T(8,128)}) custom-call(bf16[2,256,64]{2,1,0:T(8,128)(2,1)} %constant.19.clone.refs_0_, f32[3,64,128]{2,1,0:T(8,128)} %constant.20.clone.refs_1_, f32[64,128]{1,0:T(8,128)} %constant.21.clone.refs_2_, bf16[2,256,128]{2,1,0:T(8,128)(2,1)} %constant.22.clone.refs_3_, ...), custom_call_target="tpu_custom_call" | custom-call | tf_op jit(solution)/shard_map/points_basis_0/pallas_call | solution.py:249
  258.0 13.9 %all_to_all.95.refs_0_ = f32[32,16,128]{2,1,0:T(8,128)} all-to-all(f32[32,16,128]{2,1,0:T(8,128)} %bitcast.40), channel_id=1, replica_groups=mesh['modes'=8,'cheb'=4] {'modes','cheb'}, dimensions={0} | all-to-all | bytes 524288 | tf_op jit(solution)/shard_map/all_to_all | solution.py:442
  271.9 12.2 %spectral_krylov_0.3 = (f32[256,256]{1,0:T(8,128)}, f32[256,256]{1,0:T(8,128)}, f32[32,24,128]{2,1,0:T(8,128)}) custom-call(f32[32,16,128]{2,1,0:T(8,128)} %all_to_all.95.refs_0_, bf16[2,256,256]{2,1,0:T(8,128)(2,1)} %constant.18.clone.ct.refs_1_, bf16[2,256,256]{2,1,0:T(8,128)(2,1)} %constant.26.clone.refs_2_, f32[256,256]{1,0:T(8,128)} %get-tuple-element.74.refs_3_, ...), custom_call_target="tpu_custom_call" | custom-call | tf_op jit(solution)/shard_map/spectral_krylov_0/pallas_call | solution.py:385
  284.1 16.5 %all_to_all.96 = f32[32,24,128]{2,1,0:T(8,128)} all-to-all(f32[32,24,128]{2,1,0:T(8,128)} %get-tuple-element.76), channel_id=1, replica_groups=mesh['modes'=8,'cheb'=4] {'modes','cheb'}, dimensions={0} | all-to-all | bytes 786432 | tf_op jit(solution)/shard_map/all_to_all | solution.py:442
  300.6 4.5 %points_basis_1.3 = (f32[512,128]{1,0:T(8,128)}, f32[8,2,64,128]{3,2,1,0:T(8,128)}, f32[8,128]{1,0:T(8,128)}) custom-call(bf16[2,256,64]{2,1,0:T(8,128)(2,1)} %constant.19.clone.refs_0_, f32[3,64,128]{2,1,0:T(8,128)} %constant.20.clone.refs_1_, f32[64,128]{1,0:T(8,128)} %constant.21.clone.refs_2_, bf16[2,256,128]{2,1,0:T(8,128)(2,1)} %constant.22.clone.refs_3_, ...), custom_call_target="tpu_custom_call" | custom-call | tf_op jit(solution)/shard_map/points_basis_1/pallas_call | solution.py:249
  305.1 13.9 %all_to_all.97.refs_0_ = f32[32,16,128]{2,1,0:T(8,128)} all-to-all(f32[32,16,128]{2,1,0:T(8,128)} %bitcast.41), channel_id=1, replica_groups=mesh['modes'=8,'cheb'=4] {'modes','cheb'}, dimensions={0} | all-to-all | bytes 524288 | tf_op jit(solution)/shard_map/all_to_all | solution.py:442
  319.0 12.4 %spectral_krylov_1.3 = (f32[256,256]{1,0:T(8,128)}, f32[256,256]{1,0:T(8,128)}, f32[32,24,128]{2,1,0:T(8,128)}) custom-call(f32[32,16,128]{2,1,0:T(8,128)} %all_to_all.97.refs_0_, bf16[2,256,256]{2,1,0:T(8,128)(2,1)} %constant.18.clone.ct.refs_1_, bf16[2,256,256]{2,1,0:T(8,128)(2,1)} %constant.26.clone.refs_2_, f32[256,256]{1,0:T(8,128)} %get-tuple-element.79.refs_3_, ...), custom_call_target="tpu_custom_call" | custom-call | tf_op jit(solution)/shard_map/spectral_krylov_1/pallas_call | solution.py:385
  331.3 16.5 %all_to_all.98 = f32[32,24,128]{2,1,0:T(8,128)} all-to-all(f32[32,24,128]{2,1,0:T(8,128)} %get-tuple-element.82), channel_id=1, replica_groups=mesh['modes'=8,'cheb'=4] {'modes','cheb'}, dimensions={0} | all-to-all | bytes 786432 | tf_op jit(solution)/shard_map/all_to_all | solution.py:442
  347.9 4.7 %points_basis_2.3 = (f32[512,128]{1,0:T(8,128)}, f32[8,2,64,128]{3,2,1,0:T(8,128)}, f32[8,128]{1,0:T(8,128)}) custom-call(bf16[2,256,64]{2,1,0:T(8,128)(2,1)} %constant.19.clone.refs_0_, f32[3,64,128]{2,1,0:T(8,128)} %constant.20.clone.refs_1_, f32[64,128]{1,0:T(8,128)} %constant.21.clone.refs_2_, bf16[2,256,128]{2,1,0:T(8,128)(2,1)} %constant.22.clone.refs_3_, ...), custom_call_target="tpu_custom_call" | custom-call | tf_op jit(solution)/shard_map/points_basis_2/pallas_call | solution.py:249
  352.5 13.9 %all_to_all.99.refs_0_ = f32[32,16,128]{2,1,0:T(8,128)} all-to-all(f32[32,16,128]{2,1,0:T(8,128)} %bitcast.34), channel_id=1, replica_groups=mesh['modes'=8,'cheb'=4] {'modes','cheb'}, dimensions={0} | all-to-all | bytes 524288 | tf_op jit(solution)/shard_map/all_to_all | solution.py:442
  366.4 11.9 %spectral_krylov_2.3 = (f32[256,256]{1,0:T(8,128)}, f32[8,128]{1,0:T(8,128)}) custom-call(f32[32,16,128]{2,1,0:T(8,128)} %all_to_all.99.refs_0_, bf16[2,256,256]{2,1,0:T(8,128)(2,1)} %constant.18.clone.ct.refs_1_, bf16[2,256,256]{2,1,0:T(8,128)(2,1)} %constant.26.clone.refs_2_, f32[256,256]{1,0:T(8,128)} %get-tuple-element.85.refs_3_, ...), custom_call_target="tpu_custom_call" | custom-call | tf_op jit(solution)/shard_map/spectral_krylov_2/pallas_call | solution.py:385
  378.3 0.7 broadcast_in_dim.5
  379.0 10.6 %all_to_all.100.refs_0_ = f32[32,8,128]{2,1,0:T(8,128)} all-to-all(f32[32,8,128]{2,1,0:T(8,128)S(1)} %broadcast_in_dim.5), channel_id=1, replica_groups=mesh['modes'=8,'cheb'=4] {'modes','cheb'}, dimensions={0} | all-to-all | bytes 262144 | tf_op jit(solution)/shard_map/all_to_all | solution.py:442
  389.6 2.3 finish.1
  391.9 1.1 copy.23
  392.9 0.7 copy.24
Async XLA Ops:
  28.6 13.2 %all-to-all-start.1 = ((f32[32,16,128]{2,1,0:T(8,128)}), f32[32,16,128]{2,1,0:T(8,128)S(1)}, u32[]{:S(2)}, u32[]{:S(2)}) async-start(f32[32,16,128]{2,1,0:T(8,128)} %bitcast.36), calls=%async_computation.1 | async-start | bytes 524288 | tf_op jit(solution)/shard_map/all_to_all | solution.py:442
  41.8 0.7 copy-start

commit v2 on v1

--- a/solution.py
+++ b/solution.py
@@ -14,6 +14,7 @@
 AXES = ("modes", "cheb")
 F32 = jnp.float32
 BF16 = jnp.bfloat16
+GRANT = 20 * 2**20
 DOTS = 8
 
 
@@ -69,6 +70,9 @@
             partial = partial - matrix[col][row] * solved[col]
         solved[row] = partial / matrix[row][row]
     return solved
+
+
+SMALL = pltpu.CompilerParams(vmem_limit_bytes=GRANT)
 
 
 class Plan:
@@ -246,7 +250,7 @@
         else:
             send[...] = out
 
-    return pl.pallas_call(kernel, out_shape=outs, name=f"points_{mode}_{len(basis)}")(*args)
+    return pl.pallas_call(kernel, out_shape=outs, compiler_params=SMALL, name=f"points_{mode}_{len(basis)}")(*args)
 
 
 def spectral_call(plan, mode, recv, taus, states, basis=(), scal=None, emit=True):
@@ -272,9 +276,16 @@
         add(f"v{i}", v)
     if scal is not None:
         add("scal", scal)
-    names.append("taus")
-    args.append(taus)
-    specs.append(pl.BlockSpec((qb, ny, ny), lambda s: (s, 0, 0)))
+    first = not isinstance(taus, tuple)
+    if first:
+        names.append("taus")
+        args.append(pltpu.with_memory_space_constraint(taus, pltpu.HBM))
+        specs.append(pl.BlockSpec((qb, ny, ny), lambda s: (s, 0, 0)))
+    else:
+        for name, half in zip(("high", "low"), taus):
+            names.append(name)
+            args.append(half)
+            specs.append(pl.BlockSpec(memory_space=pltpu.VMEM))
 
     state_shape = jax.ShapeDtypeStruct((ny, wide), F32)
     out_names, outs = [], []
@@ -299,6 +310,10 @@
     out_specs = [
         pl.BlockSpec(o.shape, lambda s, rank=len(o.shape): (0,) * rank) for o in outs
     ]
+    if first:
+        out_names += ["high", "low"]
+        outs += [pltpu.VMEM(taus.shape, BF16)] * 2
+        out_specs += [pl.BlockSpec(memory_space=pltpu.VMEM)] * 2
 
     def kernel(*refs):
         ins = dict(zip(names, refs[: len(names)]))
@@ -328,8 +343,13 @@
             q = step * qb + t
             picked = pl.ds(q, 2 * lines // kl, stride=kl)
             rows = jnp.concatenate([c_scr[h, picked, :] for h in range(ny // 128)], axis=1).astype(BF16)
-            high, low = split(ins["taus"][t])
             dims = (((1,), (1,)), ((), ()))
+            if first:
+                high, low = split(ins["taus"][t])
+                res["high"][q] = high
+                res["low"][q] = low
+            else:
+                high, low = ins["high"][q], ins["low"][q]
             got = lax.dot_general(rows, high, dims, preferred_element_type=F32)
             got = got + lax.dot_general(rows, low, dims, preferred_element_type=F32)
             for h in range(ny // 128):
@@ -389,7 +409,9 @@
         out_specs=out_specs,
         out_shape=outs,
         scratch_shapes=[pltpu.VMEM((ny // 128, 2 * lines, 128), F32)] * 2,
-        compiler_params=pltpu.CompilerParams(dimension_semantics=("arbitrary",)),
+        compiler_params=pltpu.CompilerParams(
+            dimension_semantics=("arbitrary",), vmem_limit_bytes=GRANT
+        ),
         name=f"spectral_{mode}_{len(basis)}",
     )(*args)
     return dict(zip(out_names, got))
@@ -408,7 +430,7 @@
         out[...] = value
 
     shape = jax.ShapeDtypeStruct(iterate.shape, F32)
-    return pl.pallas_call(kernel, out_shape=shape, name="finish")(dots, ones, iterate, *basis, *scal)
+    return pl.pallas_call(kernel, out_shape=shape, compiler_params=SMALL, name="finish")(dots, ones, iterate, *basis, *scal)
 
 
 def values_call(plan, state):
@@ -429,7 +451,7 @@
         if plan.direct:
             send[:, 2 * il :, :] = jnp.zeros((group, DOTS, bq), F32)
 
-    return pl.pallas_call(kernel, out_shape=shape, name="values")(jnp.asarray(plan.ct), state)
+    return pl.pallas_call(kernel, out_shape=shape, compiler_params=SMALL, name="values")(jnp.asarray(plan.ct), state)
 
 
 def shards(start, forcing, taus):
@@ -468,6 +490,8 @@
     for newton_step in range(NEWTON):
         got = spectral_call(plan, "residual", move_back(sent), taus, (iterate, forced), basis, solved)
         iterate = got.get("iterate", iterate)
+        if "high" in got:
+            taus = (got["high"], got["low"])
         basis, basis_pts, scal = [], [], []
         for column in range(KRYLOV):
             field, dots = move_out(got["send"], got.get("dots"))

time: 396 us -> 322 us (0.81)
  Pallas kernels: 137 us -> 72.8 us
  blocking collectives: 238 us -> 224 us
  local copies, waits for them, and re-layouts: 7.48 us -> 11.9 us
    pallas_call x8, Pallas kernels: 97.7 us -> 54.4 us  [spectral_call(): pl.pallas_call(kernel, grid=(steps,), in_specs=specs, out_specs=out_specs...]
    pallas_call x10, Pallas kernels: 39.1 us -> 18.4 us  [the longest x8 17.8 us: points_call(): pl.pallas_call(kernel, out_shape=outs, compiler_params=SMALL, name=f'poin...]
    all_to_all x16, blocking collectives: 238 us -> 224 us  [swap(): return lax.all_to_all(x, AXES, split_axis=0, concat_axis=0, tiled=True)]
    unnamed x4 -> x40, local copies, waits for them, and re-layouts: 2.64 us -> 10.8 us
where the time goes in v2:
time: 322 us; the launch traced here: 321 us
  blocking collectives  224 us (70%)
  Pallas kernels  72.8 us (23%)
  local copies, waits for them, and re-layouts  11.9 us (4%)
  waiting for transfers between devices  9.46 us (3%)
    all_to_all x16, blocking collectives, swap(): return lax.all_to_all(x, AXES, split_axis=0, concat_axis=0, tiled=True)  224 us
    pallas_call x8, Pallas kernels, spectral_call(): pl.pallas_call(kernel, grid=(steps,), in_specs=specs, out_specs=out_specs...  54.4 us
    pallas_call x8, Pallas kernels, points_call(): pl.pallas_call(kernel, out_shape=outs, compiler_params=SMALL, name=f'poin...  17.8 us
    unnamed x40, local copies, waits for them, and re-layouts  10.8 us
    all_to_all x1, waiting for transfers between devices, swap(): return lax.all_to_all(x, AXES, split_axis=0, concat_axis=0, tiled=True)  9.46 us
  transfers between devices with their start and end apart: 1, of which 1 were waited for; matrix products, arithmetic and copies ran while one was open for 0% of the time, Pallas kernels for 0%

profile of v2, /device:TPU:0, one launch (start us, length us, event | category | flops | bytes accessed | tf_op | source)
XLA Modules:
  0.0 320.7 jit_solution(11007317220749254519)
XLA Ops:
  0.0 1.0 copy.16
  1.1 0.9 copy-done
  2.3 20.4 %all_to_all.85 = f32[32,24,128]{2,1,0:T(8,128)S(1)} all-to-all(f32[32,24,128]{2,1,0:T(8,128)S(1)} %values.1), channel_id=1, replica_groups=mesh['modes'=8,'cheb'=4] {'modes','cheb'}, dimensions={0} | all-to-all | bytes 786432 | tf_op jit(solution)/shard_map/all_to_all | solution.py:464
  22.7 0.9 copy-done.5
  23.6 0.9 copy-done.7
  24.5 0.9 copy-done.9
  25.4 0.9 copy-done.11
  26.3 0.8 copy-done.13
  27.2 0.8 copy-done.15
  27.9 0.8 copy-done.17
  28.7 2.8 points_start_0.1
  31.5 2.6 all-to-all-start.1
  34.1 1.0 copy.18
  35.2 9.5 %all-to-all-done.1.refs_0_ = f32[32,16,128]{2,1,0:T(8,128)S(1)} async-done(((f32[32,16,128]{2,1,0:T(8,128)}), f32[32,16,128]{2,1,0:T(8,128)S(1)}, u32[]{:S(2)}, u32[]{:S(2)}) %all-to-all-start.1) | async-done | bytes 262176 | tf_op jit(solution)/shard_map/all_to_all | solution.py:464
  44.6 0.9 copy-done.1
  45.6 0.9 copy-done.3
  46.6 11.4 %spectral_residual_0.1 = (f32[256,256]{1,0:T(8,128)S(1)}, f32[32,24,128]{2,1,0:T(8,128)S(1)}, bf16[64,256,256]{2,1,0:T(8,128)(2,1)S(1)}, bf16[64,256,256]{2,1,0:T(8,128)(2,1)S(1)}) custom-call(f32[32,16,128]{2,1,0:T(8,128)S(1)} %all-to-all-done.1.refs_0_, bf16[2,256,256]{2,1,0:T(8,128)(2,1)S(1)} %copy-done.1, bf16[2,256,256]{2,1,0:T(8,128)(2,1)S(1)} %copy-done.3, ...), custom_call_target="tpu_custom_call" | custom-call | tf_op jit(solution)/shard_map/spectral_residual_0/pallas_call | solution.py:405
  58.0 15.4 %all_to_all.86 = f32[32,24,128]{2,1,0:T(8,128)S(1)} all-to-all(f32[32,24,128]{2,1,0:T(8,128)S(1)} %get-tuple-element.51), channel_id=1, replica_groups=mesh['modes'=8,'cheb'=4] {'modes','cheb'}, dimensions={0} | all-to-all | bytes 786432 | tf_op jit(solution)/shard_map/all_to_all | solution.py:464
  73.4 2.2 points_basis_0.2
  75.7 12.9 %all_to_all.87.refs_0_ = f32[32,16,128]{2,1,0:T(8,128)S(1)} all-to-all(f32[32,16,128]{2,1,0:T(8,128)S(1)} %bitcast.33), channel_id=1, replica_groups=mesh['modes'=8,'cheb'=4] {'modes','cheb'}, dimensions={0} | all-to-all | bytes 524288 | tf_op jit(solution)/shard_map/all_to_all | solution.py:464
  88.6 6.2 %spectral_krylov_0.2 = (f32[256,256]{1,0:T(8,128)S(1)}, f32[256,256]{1,0:T(8,128)S(1)}, f32[32,24,128]{2,1,0:T(8,128)S(1)}) custom-call(f32[32,16,128]{2,1,0:T(8,128)S(1)} %all_to_all.87.refs_0_, bf16[2,256,256]{2,1,0:T(8,128)(2,1)S(1)} %copy-done.2, bf16[2,256,256]{2,1,0:T(8,128)(2,1)S(1)} %copy-done.4, f32[256,256]{1,0:T(8,128)S(1)} %get-tuple-element.54.refs_3_, ...), custom_call_target="tpu_custom_call" | custom-call | tf_op jit(solution)/shard_map/spectral_krylov_0/pallas_call | solution.py:405
  94.8 15.4 %all_to_all.88 = f32[32,24,128]{2,1,0:T(8,128)S(1)} all-to-all(f32[32,24,128]{2,1,0:T(8,128)S(1)} %get-tuple-element.58), channel_id=1, replica_groups=mesh['modes'=8,'cheb'=4] {'modes','cheb'}, dimensions={0} | all-to-all | bytes 786432 | tf_op jit(solution)/shard_map/all_to_all | solution.py:464
  110.2 2.2 points_basis_1.2
  112.5 12.9 %all_to_all.89.refs_0_ = f32[32,16,128]{2,1,0:T(8,128)S(1)} all-to-all(f32[32,16,128]{2,1,0:T(8,128)S(1)} %bitcast.34), channel_id=1, replica_groups=mesh['modes'=8,'cheb'=4] {'modes','cheb'}, dimensions={0} | all-to-all | bytes 524288 | tf_op jit(solution)/shard_map/all_to_all | solution.py:464
  125.4 6.2 %spectral_krylov_1.2 = (f32[256,256]{1,0:T(8,128)S(1)}, f32[256,256]{1,0:T(8,128)S(1)}, f32[32,24,128]{2,1,0:T(8,128)S(1)}) custom-call(f32[32,16,128]{2,1,0:T(8,128)S(1)} %all_to_all.89.refs_0_, bf16[2,256,256]{2,1,0:T(8,128)(2,1)S(1)} %copy-done.2, bf16[2,256,256]{2,1,0:T(8,128)(2,1)S(1)} %copy-done.4, f32[256,256]{1,0:T(8,128)S(1)} %get-tuple-element.61.refs_3_, ...), custom_call_target="tpu_custom_call" | custom-call | tf_op jit(solution)/shard_map/spectral_krylov_1/pallas_call | solution.py:405
  131.6 15.4 %all_to_all.90 = f32[32,24,128]{2,1,0:T(8,128)S(1)} all-to-all(f32[32,24,128]{2,1,0:T(8,128)S(1)} %get-tuple-element.64), channel_id=1, replica_groups=mesh['modes'=8,'cheb'=4] {'modes','cheb'}, dimensions={0} | all-to-all | bytes 786432 | tf_op jit(solution)/shard_map/all_to_all | solution.py:464
  147.1 2.2 points_basis_2.2
  149.3 12.9 %all_to_all.91.refs_0_ = f32[32,16,128]{2,1,0:T(8,128)S(1)} all-to-all(f32[32,16,128]{2,1,0:T(8,128)S(1)} %bitcast.35), channel_id=1, replica_groups=mesh['modes'=8,'cheb'=4] {'modes','cheb'}, dimensions={0} | all-to-all | bytes 524288 | tf_op jit(solution)/shard_map/all_to_all | solution.py:464
  162.2 6.0 %spectral_krylov_2.2 = (f32[256,256]{1,0:T(8,128)S(1)}, f32[8,128]{1,0:T(8,128)S(1)}) custom-call(f32[32,16,128]{2,1,0:T(8,128)S(1)} %all_to_all.91.refs_0_, bf16[2,256,256]{2,1,0:T(8,128)(2,1)S(1)} %copy-done.2, bf16[2,256,256]{2,1,0:T(8,128)(2,1)S(1)} %copy-done.4, f32[256,256]{1,0:T(8,128)S(1)} %get-tuple-element.67.refs_3_, ...), custom_call_target="tpu_custom_call" | custom-call | tf_op jit(solution)/shard_map/spectral_krylov_2/pallas_call | solution.py:405
  168.2 10.4 %all_to_all.92.refs_7_ = f32[32,8,128]{2,1,0:T(8,128)S(1)} all-to-all(f32[32,8,128]{2,1,0:T(8,128)S(1)} %broadcast_in_dim.4), channel_id=1, replica_groups=mesh['modes'=8,'cheb'=4] {'modes','cheb'}, dimensions={0} | all-to-all | bytes 262144 | tf_op jit(solution)/shard_map/all_to_all | solution.py:464
  178.6 1.1 points_restart_3.1
  179.8 12.3 %all_to_all.93.refs_0_ = f32[32,16,128]{2,1,0:T(8,128)S(1)} all-to-all(f32[32,16,128]{2,1,0:T(8,128)S(1)} %bitcast.32), channel_id=1, replica_groups=mesh['modes'=8,'cheb'=4] {'modes','cheb'}, dimensions={0} | all-to-all | bytes 524288 | tf_op jit(solution)/shard_map/all_to_all | solution.py:464
  192.1 6.2 %spectral_residual_3.1 = (f32[256,256]{1,0:T(8,128)S(1)}, f32[256,256]{1,0:T(8,128)S(1)}, f32[32,24,128]{2,1,0:T(8,128)S(1)}) custom-call(f32[32,16,128]{2,1,0:T(8,128)S(1)} %all_to_all.93.refs_0_, bf16[2,256,256]{2,1,0:T(8,128)(2,1)S(1)} %copy-done.2, bf16[2,256,256]{2,1,0:T(8,128)(2,1)S(1)} %copy-done.4, f32[256,256]{1,0:T(8,128)S(1)} %copy.17.x.refs_3_, ...), custom_call_target="tpu_custom_call" | custom-call | tf_op jit(solution)/shard_map/spectral_residual_3/pallas_call | solution.py:405
  198.3 15.4 %all_to_all.94 = f32[32,24,128]{2,1,0:T(8,128)S(1)} all-to-all(f32[32,24,128]{2,1,0:T(8,128)S(1)} %get-tuple-element.75), channel_id=1, replica_groups=mesh['modes'=8,'cheb'=4] {'modes','cheb'}, dimensions={0} | all-to-all | bytes 786432 | tf_op jit(solution)/shard_map/all_to_all | solution.py:464
  213.8 2.2 points_basis_0.3
  216.0 12.9 %all_to_all.95.refs_0_ = f32[32,16,128]{2,1,0:T(8,128)S(1)} all-to-all(f32[32,16,128]{2,1,0:T(8,128)S(1)} %bitcast.36), channel_id=1, replica_groups=mesh['modes'=8,'cheb'=4] {'modes','cheb'}, dimensions={0} | all-to-all | bytes 524288 | tf_op jit(solution)/shard_map/all_to_all | solution.py:464
  228.9 6.2 %spectral_krylov_0.3 = (f32[256,256]{1,0:T(8,128)S(1)}, f32[256,256]{1,0:T(8,128)S(1)}, f32[32,24,128]{2,1,0:T(8,128)S(1)}) custom-call(f32[32,16,128]{2,1,0:T(8,128)S(1)} %all_to_all.95.refs_0_, bf16[2,256,256]{2,1,0:T(8,128)(2,1)S(1)} %copy-done.2, bf16[2,256,256]{2,1,0:T(8,128)(2,1)S(1)} %copy-done.4, f32[256,256]{1,0:T(8,128)S(1)} %get-tuple-element.78.refs_3_, ...), custom_call_target="tpu_custom_call" | custom-call | tf_op jit(solution)/shard_map/spectral_krylov_0/pallas_call | solution.py:405
  235.1 15.4 %all_to_all.96 = f32[32,24,128]{2,1,0:T(8,128)S(1)} all-to-all(f32[32,24,128]{2,1,0:T(8,128)S(1)} %get-tuple-element.80), channel_id=1, replica_groups=mesh['modes'=8,'cheb'=4] {'modes','cheb'}, dimensions={0} | all-to-all | bytes 786432 | tf_op jit(solution)/shard_map/all_to_all | solution.py:464
  250.6 2.2 points_basis_1.3
  252.8 12.9 %all_to_all.97.refs_0_ = f32[32,16,128]{2,1,0:T(8,128)S(1)} all-to-all(f32[32,16,128]{2,1,0:T(8,128)S(1)} %bitcast.37), channel_id=1, replica_groups=mesh['modes'=8,'cheb'=4] {'modes','cheb'}, dimensions={0} | all-to-all | bytes 524288 | tf_op jit(solution)/shard_map/all_to_all | solution.py:464
  265.7 6.2 %spectral_krylov_1.3 = (f32[256,256]{1,0:T(8,128)S(1)}, f32[256,256]{1,0:T(8,128)S(1)}, f32[32,24,128]{2,1,0:T(8,128)S(1)}) custom-call(f32[32,16,128]{2,1,0:T(8,128)S(1)} %all_to_all.97.refs_0_, bf16[2,256,256]{2,1,0:T(8,128)(2,1)S(1)} %copy-done.2, bf16[2,256,256]{2,1,0:T(8,128)(2,1)S(1)} %copy-done.4, f32[256,256]{1,0:T(8,128)S(1)} %get-tuple-element.83.refs_3_, ...), custom_call_target="tpu_custom_call" | custom-call | tf_op jit(solution)/shard_map/spectral_krylov_1/pallas_call | solution.py:405
  272.0 15.5 %all_to_all.98 = f32[32,24,128]{2,1,0:T(8,128)S(1)} all-to-all(f32[32,24,128]{2,1,0:T(8,128)S(1)} %get-tuple-element.86), channel_id=1, replica_groups=mesh['modes'=8,'cheb'=4] {'modes','cheb'}, dimensions={0} | all-to-all | bytes 786432 | tf_op jit(solution)/shard_map/all_to_all | solution.py:464
  287.4 2.8 points_basis_2.3
  290.2 12.9 %all_to_all.99.refs_0_ = f32[32,16,128]{2,1,0:T(8,128)S(1)} all-to-all(f32[32,16,128]{2,1,0:T(8,128)S(1)} %bitcast.31), channel_id=1, replica_groups=mesh['modes'=8,'cheb'=4] {'modes','cheb'}, dimensions={0} | all-to-all | bytes 524288 | tf_op jit(solution)/shard_map/all_to_all | solution.py:464
  303.1 6.0 %spectral_krylov_2.3 = (f32[256,256]{1,0:T(8,128)S(1)}, f32[8,128]{1,0:T(8,128)S(1)}) custom-call(f32[32,16,128]{2,1,0:T(8,128)S(1)} %all_to_all.99.refs_0_, bf16[2,256,256]{2,1,0:T(8,128)(2,1)S(1)} %copy-done.2, bf16[2,256,256]{2,1,0:T(8,128)(2,1)S(1)} %copy-done.4, f32[256,256]{1,0:T(8,128)S(1)} %get-tuple-element.89.refs_3_, ...), custom_call_target="tpu_custom_call" | custom-call | tf_op jit(solution)/shard_map/spectral_krylov_2/pallas_call | solution.py:405
  309.1 10.4 %all_to_all.100.refs_0_ = f32[32,8,128]{2,1,0:T(8,128)S(1)} all-to-all(f32[32,8,128]{2,1,0:T(8,128)S(1)} %broadcast_in_dim.5), channel_id=1, replica_groups=mesh['modes'=8,'cheb'=4] {'modes','cheb'}, dimensions={0} | all-to-all | bytes 262144 | tf_op jit(solution)/shard_map/all_to_all | solution.py:464
  319.5 0.3 finish.1
  319.9 0.7 copy.24
  (34 shorter events, 0.7 us)
Async XLA Ops:
  1.1 1.0 copy-start
  22.7 0.9 copy-start.5
  23.6 0.9 copy-start.7
  24.5 0.9 copy-start.9
  25.4 0.9 copy-start.11
  26.3 0.8 copy-start.13
  27.2 0.8 copy-start.15
  27.9 0.8 copy-start.17
  31.5 13.2 %all-to-all-start.1 = ((f32[32,16,128]{2,1,0:T(8,128)}), f32[32,16,128]{2,1,0:T(8,128)S(1)}, u32[]{:S(2)}, u32[]{:S(2)}) async-start(f32[32,16,128]{2,1,0:T(8,128)} %bitcast.3), calls=%async_computation.1 | async-start | bytes 524288 | tf_op jit(solution)/shard_map/all_to_all | solution.py:464
  44.6 1.0 copy-start.1
  45.6 0.9 copy-start.3
  46.5 26.9 %copy-start.6 = (bf16[2,128,256]{2,1,0:T(8,128)(2,1)S(1)}, bf16[2,128,256]{2,1,0:T(8,128)(2,1)}, u32[]{:S(2)}) copy-start(bf16[2,128,256]{2,1,0:T(8,128)(2,1)} %constant.23.clone.refs_4_) | copy-start | bytes 393220
  46.5 26.9 %copy-start.8 = (bf16[2,256,128]{2,1,0:T(8,128)(2,1)S(1)}, bf16[2,256,128]{2,1,0:T(8,128)(2,1)}, u32[]{:S(2)}) copy-start(bf16[2,256,128]{2,1,0:T(8,128)(2,1)} %constant.22.clone.refs_3_) | copy-start | bytes 393220
  46.5 26.9 %copy-start.10 = (bf16[2,256,64]{2,1,0:T(8,128)(2,1)S(1)}, bf16[2,256,64]{2,1,0:T(8,128)(2,1)}, u32[]{:S(2)}) copy-start(bf16[2,256,64]{2,1,0:T(8,128)(2,1)} %constant.19.clone.refs_0_) | copy-start | bytes 196612
  46.5 26.9 %copy-start.12 = (f32[3,64,128]{2,1,0:T(8,128)S(1)}, f32[3,64,128]{2,1,0:T(8,128)}, u32[]{:S(2)}) copy-start(f32[3,64,128]{2,1,0:T(8,128)} %constant.20.clone.refs_1_) | copy-start | bytes 294916
  46.5 26.9 %copy-start.14 = (f32[128,128]{1,0:T(8,128)S(1)}, f32[128,128]{1,0:T(8,128)}, u32[]{:S(2)}) copy-start(f32[128,128]{1,0:T(8,128)} %constant.25.clone.refs_6_.refs_1_) | copy-start | bytes 196612
  46.6 26.9 %copy-start.16 = (bf16[2,64,128]{2,1,0:T(8,128)(2,1)S(1)}, bf16[2,64,128]{2,1,0:T(8,128)(2,1)}, u32[]{:S(2)}) copy-start(bf16[2,64,128]{2,1,0:T(8,128)(2,1)} %constant.24.clone.refs_5_) | copy-start | bytes 98308
  46.6 26.9 %copy-start.18 = (f32[64,128]{1,0:T(8,128)S(1)}, f32[64,128]{1,0:T(8,128)}, u32[]{:S(2)}) copy-start(f32[64,128]{1,0:T(8,128)} %constant.21.clone.refs_2_) | copy-start | bytes 98308
  46.6 42.0 %copy-start.2 = (bf16[2,256,256]{2,1,0:T(8,128)(2,1)S(1)}, bf16[2,256,256]{2,1,0:T(8,128)(2,1)}, u32[]{:S(2)}) copy-start(bf16[2,256,256]{2,1,0:T(8,128)(2,1)} %constant.18.clone.ct.refs_1_) | copy-start | bytes 786436
  46.6 42.0 %copy-start.4 = (bf16[2,256,256]{2,1,0:T(8,128)(2,1)S(1)}, bf16[2,256,256]{2,1,0:T(8,128)(2,1)}, u32[]{:S(2)}) copy-start(bf16[2,256,256]{2,1,0:T(8,128)(2,1)} %constant.26.clone.refs_2_) | copy-start | bytes 786436

commit v3 on v2

--- a/solution.py
+++ b/solution.py
@@ -23,6 +23,10 @@
     high = table.astype(BF16)
     low = (table - high.astype(np.float32)).astype(BF16)
     return np.stack([high, low])
+
+
+def from_hbm(x):
+    return pltpu.with_memory_space_constraint(x, pltpu.HBM)
 
 
 def split(x):
@@ -118,9 +122,24 @@
         return [self.t1, self.tw, self.wt, self.b2, self.b3, self.t4, self.ones]
 
 
-def flow_sums(dots, ones_ref):
-    total = jnp.sum(dots, axis=0)
-    return jnp.dot(total, ones_ref[...], precision=lax.Precision.HIGHEST, preferred_element_type=F32)
+def over_modes(dots, ones_ref):
+    return jnp.dot(dots, ones_ref[...], precision=lax.Precision.HIGHEST, preferred_element_type=F32)
+
+
+def pack_dots(lanes, ones_ref, kl):
+    bq = lanes[0].shape[1]
+    lanes = lanes + [jnp.zeros((1, bq), F32)] * (DOTS - len(lanes))
+    sums = over_modes(jnp.concatenate(lanes, axis=0), ones_ref)
+    row_of = lax.broadcasted_iota(jnp.int32, sums.shape, 0)
+    lane = lax.broadcasted_iota(jnp.int32, sums.shape, 1)
+    return jnp.sum(jnp.where(lane % kl == row_of, sums, 0.0), axis=0, keepdims=True)
+
+
+def flow_sums(rows, ones_ref, kl):
+    total = jnp.broadcast_to(jnp.sum(rows, axis=0, keepdims=True), (DOTS, rows.shape[1]))
+    row_of = lax.broadcasted_iota(jnp.int32, total.shape, 0)
+    lane = lax.broadcasted_iota(jnp.int32, total.shape, 1)
+    return over_modes(jnp.where(lane % kl == row_of, total, 0.0), ones_ref)
 
 
 def new_column(sums, count):
@@ -145,7 +164,7 @@
 
 def points_call(plan, mode, field=None, dots=None, base=None, basis=(), scal=()):
     group, il, bq, j1 = plan.group, plan.il, plan.bq, plan.j1
-    stride_in, stride_out = 2 * il + DOTS, 2 * il
+    stride_in, stride_out = 2 * il + (mode == "basis"), 2 * il
     names, args = [], []
 
     def add(name, value):
@@ -153,7 +172,8 @@
         args.append(value)
 
     for name, value in zip(("t1", "tw", "wt", "b2", "b3", "t4", "ones"), plan.tables()):
-        add(name, jnp.asarray(value))
+        value = jnp.asarray(value)
+        add(name, from_hbm(value) if mode == "start" else value)
     if field is not None:
         add("field", field)
     if dots is not None:
@@ -209,10 +229,10 @@
             product = pts[:, 0] * pts[:, 1]
         elif mode == "basis":
             if plan.direct:
-                parts = ins["field"][...].reshape(group, stride_in, bq)[:, 2 * il :, :]
+                parts = ins["field"][pl.ds(2 * il, group, stride=stride_in), :]
             else:
                 parts = ins["dots"][...]
-            sums = flow_sums(parts, ins["ones"])
+            sums = flow_sums(parts, ins["ones"], plan.kl)
             pts = to_points()
             if not basis:
                 column = [jnp.sqrt(sums[0:1])]
@@ -226,7 +246,7 @@
             pts_out[...] = pts
             product = ins["base"][:, 0] * pts[:, 1] + pts[:, 0] * ins["base"][:, 1]
         else:
-            sums = flow_sums(ins["dots"][...], ins["ones"])
+            sums = flow_sums(ins["dots"][...], ins["ones"], plan.kl)
             solved = solve_rows(sums, [ins[f"s{i}"][...] for i in range(KRYLOV)])
             pts = ins["base"][...]
             for i in range(KRYLOV):
@@ -268,18 +288,19 @@
         specs.append(pl.BlockSpec(value.shape, lambda s, rank=rank: (0,) * rank))
 
     add("recv", recv)
-    add("ct", jnp.asarray(plan.ct))
-    add("cw", jnp.asarray(plan.cw))
+    first = not isinstance(taus, tuple)
+    for name, value in (("ct", plan.ct), ("cw", plan.cw), ("ones", plan.ones)):
+        value = jnp.asarray(value)
+        add(name, from_hbm(value) if first else value)
     for i, v in enumerate(states):
         add(f"x{i}", v)
     for i, v in enumerate(basis):
         add(f"v{i}", v)
     if scal is not None:
         add("scal", scal)
-    first = not isinstance(taus, tuple)
     if first:
         names.append("taus")
-        args.append(pltpu.with_memory_space_constraint(taus, pltpu.HBM))
+        args.append(from_hbm(taus))
         specs.append(pl.BlockSpec((qb, ny, ny), lambda s: (s, 0, 0)))
     else:
         for name, half in zip(("high", "low"), taus):
@@ -301,12 +322,12 @@
         outs.append(state_shape)
         out_names.append("send")
         if plan.direct:
-            outs.append(jax.ShapeDtypeStruct((group, 2 * il + DOTS, bq), F32))
+            outs.append(jax.ShapeDtypeStruct((group * (2 * il + 1), bq), F32))
         else:
             outs.append(jax.ShapeDtypeStruct((2, ny, bq), F32))
     if not (emit and plan.direct):
         out_names.append("dots")
-        outs.append(jax.ShapeDtypeStruct((DOTS, bq), F32))
+        outs.append(jax.ShapeDtypeStruct((group, bq), F32))
     out_specs = [
         pl.BlockSpec(o.shape, lambda s, rank=len(o.shape): (0,) * rank) for o in outs
     ]
@@ -386,19 +407,20 @@
             for other in others + [applied]:
                 dot = jnp.sum(other * applied, axis=0, keepdims=True)
                 lanes.append(dot[:, :bq] + dot[:, bq:])
-            lanes += [jnp.zeros((1, bq), F32)] * (DOTS - len(lanes))
-            dots = jnp.concatenate(lanes, axis=0)
+            dots = jnp.broadcast_to(pack_dots(lanes, ins["ones"], kl), (group, bq))
             if emit:
                 res["applied"][...] = applied
                 values = table_left(ins["ct"], applied)
                 for r in range(2):
                     side = values[:, r * bq : (r + 1) * bq]
                     if plan.direct:
-                        res["send"][:, r * il : (r + 1) * il, :] = side.reshape(group, il, bq)
+                        for e in range(group):
+                            at = e * (2 * il + 1) + r * il
+                            res["send"][at : at + il, :] = side[e * il : (e + 1) * il]
                     else:
                         res["send"][r] = side
             if emit and plan.direct:
-                res["send"][:, 2 * il :, :] = jnp.broadcast_to(dots[None], (group, DOTS, bq))
+                res["send"][pl.ds(2 * il, group, stride=2 * il + 1), :] = dots
             else:
                 res["dots"][...] = dots
 
@@ -422,7 +444,7 @@
 
     def kernel(*refs):
         out = refs[-1]
-        sums = flow_sums(refs[0][...], refs[1])
+        sums = flow_sums(refs[0][...], refs[1], plan.kl)
         solved = solve_rows(sums, [r[...] for r in refs[3 + KRYLOV : 3 + 2 * KRYLOV]])
         value = refs[2][...]
         for i in range(KRYLOV):
@@ -436,7 +458,7 @@
 def values_call(plan, state):
     group, il, bq, ny = plan.group, plan.il, plan.bq, plan.ny
     if plan.direct:
-        shape = jax.ShapeDtypeStruct((group, 2 * il + DOTS, bq), F32)
+        shape = jax.ShapeDtypeStruct((group, 2 * il, bq), F32)
     else:
         shape = jax.ShapeDtypeStruct((2, ny, bq), F32)
 
@@ -448,10 +470,10 @@
                 send[:, r * il : (r + 1) * il, :] = side.reshape(group, il, bq)
             else:
                 send[r] = side
-        if plan.direct:
-            send[:, 2 * il :, :] = jnp.zeros((group, DOTS, bq), F32)
-
-    return pl.pallas_call(kernel, out_shape=shape, compiler_params=SMALL, name="values")(jnp.asarray(plan.ct), state)
+
+    return pl.pallas_call(kernel, out_shape=shape, compiler_params=SMALL, name="values")(
+        from_hbm(jnp.asarray(plan.ct)), state
+    )
 
 
 def shards(start, forcing, taus):
@@ -464,12 +486,13 @@
         return lax.all_to_all(x, AXES, split_axis=0, concat_axis=0, tiled=True)
 
     def gather_dots(dots):
-        return swap(jnp.broadcast_to(dots[None], (group,) + dots.shape))
+        return swap(dots.reshape(group, 1, bq)).reshape(group, bq)
 
     def move_out(sent, dots=None):
         if plan.direct:
-            got = swap(sent)
-            return got.reshape(group * (2 * il + DOTS), bq), None
+            if sent.ndim == 2:
+                sent = sent.reshape(group, 1, -1)
+            return swap(sent).reshape(-1, bq), None
         blocks = sent.reshape(2, group, il, bq).transpose(1, 0, 2, 3).reshape(group, 2 * il, bq)
         got = swap(blocks).reshape(group, 2, il, bq).transpose(1, 0, 2, 3)
         return got.reshape(2 * group, il * bq), None if dots is None else gather_dots(dots)

time: 322 us -> 295 us (0.916)
  blocking collectives: 224 us -> 204 us
  local copies, waits for them, and re-layouts: 11.9 us -> 3.11 us
    all_to_all x16, blocking collectives: 224 us -> 204 us  [swap(): return lax.all_to_all(x, AXES, split_axis=0, concat_axis=0, tiled=True)]
    unnamed x40 -> x20, local copies, waits for them, and re-layouts: 10.8 us -> 2 us
where the time goes in v3:
time: 295 us
  blocking collectives  204 us (69%)
  Pallas kernels  75.4 us (26%)
  waiting for transfers between devices  9.35 us (3%)
  local copies, waits for them, and re-layouts  3.11 us (1%)
    all_to_all x16, blocking collectives, swap(): return lax.all_to_all(x, AXES, split_axis=0, concat_axis=0, tiled=True)  204 us
    pallas_call x8, Pallas kernels, spectral_call(): pl.pallas_call(kernel, grid=(steps,), in_specs=specs, out_specs=out_specs...  55.1 us
    pallas_call x8, Pallas kernels, points_call(): pl.pallas_call(kernel, out_shape=outs, compiler_params=SMALL, name=f'poin...  18.8 us
    all_to_all x1, waiting for transfers between devices, swap(): return lax.all_to_all(x, AXES, split_axis=0, concat_axis=0, tiled=True)  9.35 us
  transfers between devices with their start and end apart: 1, of which 1 were waited for; matrix products, arithmetic and copies ran while one was open for 0% of the time, Pallas kernels for 0%

profile of v3, /device:TPU:0, one launch (start us, length us, event | category | flops | bytes accessed | tf_op | source)
XLA Modules:
  0.0 294.7 jit_solution(87658139773901089)
XLA Ops:
  0.0 1.0 copy.25
  1.0 0.1 copy.26.x.refs_4_
  1.1 1.2 values.1
  2.3 17.7 %all_to_all.85 = f32[32,16,128]{2,1,0:T(8,128)S(1)} all-to-all(f32[32,16,128]{2,1,0:T(8,128)S(1)} %values.1), channel_id=1, replica_groups=mesh['modes'=8,'cheb'=4] {'modes','cheb'}, dimensions={0} | all-to-all | bytes 524288 | tf_op jit(solution)/shard_map/all_to_all | solution.py:486
  20.0 3.9 %points_start_0.1 = (f32[512,128]{1,0:T(8,128)}, f32[8,2,64,128]{3,2,1,0:T(8,128)S(1)}) custom-call(bf16[2,256,64]{2,1,0:T(8,128)(2,1)} %constant.19.clone.refs_0_, f32[3,64,128]{2,1,0:T(8,128)} %constant.20.clone.refs_1_, f32[64,128]{1,0:T(8,128)} %constant.21.clone.refs_2_, bf16[2,256,128]{2,1,0:T(8,128)(2,1)} %constant.22.clone.refs_3_, ...), custom_call_target="tpu_custom_call" | custom-call | tf_op jit(solution)/shard_map/points_start_0/pallas_call | solution.py:273
  24.0 2.6 all-to-all-start.1
  26.6 1.0 copy.27
  27.5 0.1 copy.29.refs_5_
  27.7 0.0 copy-start.1
  27.7 0.0 copy-start.3
  27.7 0.0 copy-start.5
  27.7 0.0 copy-start.6
  27.7 0.0 copy-start.7
  27.7 0.0 copy-start.8
  27.8 9.3 %all-to-all-done.1.refs_0_ = f32[32,16,128]{2,1,0:T(8,128)S(1)} async-done(((f32[32,16,128]{2,1,0:T(8,128)}), f32[32,16,128]{2,1,0:T(8,128)S(1)}, u32[]{:S(2)}, u32[]{:S(2)}) %all-to-all-start.1) | async-done | bytes 262176 | tf_op jit(solution)/shard_map/all_to_all | solution.py:486
  37.1 11.4 %spectral_residual_0.1 = (f32[256,256]{1,0:T(8,128)S(1)}, f32[544,128]{1,0:T(8,128)S(1)}, bf16[64,256,256]{2,1,0:T(8,128)(2,1)S(1)}, bf16[64,256,256]{2,1,0:T(8,128)(2,1)S(1)}) custom-call(f32[32,16,128]{2,1,0:T(8,128)S(1)} %all-to-all-done.1.refs_0_, bf16[2,256,256]{2,1,0:T(8,128)(2,1)} %constant.18.clone.ct.refs_1_, ...), custom_call_target="tpu_custom_call" | custom-call | tf_op jit(solution)/shard_map/spectral_residual_0/pallas_call | solution.py:427
  48.6 13.2 %all_to_all.86 = f32[32,1,2176]{2,1,0:T(1,128)S(1)} all-to-all(f32[32,1,2176]{2,1,0:T(1,128)S(1)} %bitcast.46), channel_id=1, replica_groups=mesh['modes'=8,'cheb'=4] {'modes','cheb'}, dimensions={0} | all-to-all | bytes 557056 | tf_op jit(solution)/shard_map/all_to_all | solution.py:486
  61.8 2.2 points_basis_0.2
  64.0 12.6 %all_to_all.87.refs_0_ = f32[32,16,128]{2,1,0:T(8,128)S(1)} all-to-all(f32[32,16,128]{2,1,0:T(8,128)S(1)} %bitcast.53), channel_id=1, replica_groups=mesh['modes'=8,'cheb'=4] {'modes','cheb'}, dimensions={0} | all-to-all | bytes 524288 | tf_op jit(solution)/shard_map/all_to_all | solution.py:486
  76.7 6.3 %spectral_krylov_0.2 = (f32[256,256]{1,0:T(8,128)S(1)}, f32[256,256]{1,0:T(8,128)S(1)}, f32[544,128]{1,0:T(8,128)S(1)}) custom-call(f32[32,16,128]{2,1,0:T(8,128)S(1)} %all_to_all.87.refs_0_, bf16[2,256,256]{2,1,0:T(8,128)(2,1)S(1)} %copy-done, bf16[2,256,256]{2,1,0:T(8,128)(2,1)S(1)} %copy-done.2, f32[128,128]{1,0:T(8,128)S(1)} %copy-done.1, ...), custom_call_target="tpu_custom_call" | custom-call | tf_op jit(solution)/shard_map/spectral_krylov_0/pallas_call | solution.py:427
  82.9 13.3 %all_to_all.88 = f32[32,1,2176]{2,1,0:T(1,128)S(1)} all-to-all(f32[32,1,2176]{2,1,0:T(1,128)S(1)} %bitcast.47), channel_id=1, replica_groups=mesh['modes'=8,'cheb'=4] {'modes','cheb'}, dimensions={0} | all-to-all | bytes 557056 | tf_op jit(solution)/shard_map/all_to_all | solution.py:486
  96.2 2.2 points_basis_1.2
  98.4 12.6 %all_to_all.89.refs_0_ = f32[32,16,128]{2,1,0:T(8,128)S(1)} all-to-all(f32[32,16,128]{2,1,0:T(8,128)S(1)} %bitcast.54), channel_id=1, replica_groups=mesh['modes'=8,'cheb'=4] {'modes','cheb'}, dimensions={0} | all-to-all | bytes 524288 | tf_op jit(solution)/shard_map/all_to_all | solution.py:486
  111.1 6.3 %spectral_krylov_1.2 = (f32[256,256]{1,0:T(8,128)S(1)}, f32[256,256]{1,0:T(8,128)S(1)}, f32[544,128]{1,0:T(8,128)S(1)}) custom-call(f32[32,16,128]{2,1,0:T(8,128)S(1)} %all_to_all.89.refs_0_, bf16[2,256,256]{2,1,0:T(8,128)(2,1)S(1)} %copy-done, bf16[2,256,256]{2,1,0:T(8,128)(2,1)S(1)} %copy-done.2, f32[128,128]{1,0:T(8,128)S(1)} %copy-done.1, ...), custom_call_target="tpu_custom_call" | custom-call | tf_op jit(solution)/shard_map/spectral_krylov_1/pallas_call | solution.py:427
  117.4 13.3 %all_to_all.90 = f32[32,1,2176]{2,1,0:T(1,128)S(1)} all-to-all(f32[32,1,2176]{2,1,0:T(1,128)S(1)} %bitcast.48), channel_id=1, replica_groups=mesh['modes'=8,'cheb'=4] {'modes','cheb'}, dimensions={0} | all-to-all | bytes 557056 | tf_op jit(solution)/shard_map/all_to_all | solution.py:486
  130.6 2.2 points_basis_2.2
  132.8 12.6 %all_to_all.91.refs_0_ = f32[32,16,128]{2,1,0:T(8,128)S(1)} all-to-all(f32[32,16,128]{2,1,0:T(8,128)S(1)} %bitcast.55), channel_id=1, replica_groups=mesh['modes'=8,'cheb'=4] {'modes','cheb'}, dimensions={0} | all-to-all | bytes 524288 | tf_op jit(solution)/shard_map/all_to_all | solution.py:486
  145.5 6.1 %spectral_krylov_2.2 = (f32[256,256]{1,0:T(8,128)S(1)}, f32[32,128]{1,0:T(8,128)S(1)}) custom-call(f32[32,16,128]{2,1,0:T(8,128)S(1)} %all_to_all.91.refs_0_, bf16[2,256,256]{2,1,0:T(8,128)(2,1)S(1)} %copy-done, bf16[2,256,256]{2,1,0:T(8,128)(2,1)S(1)} %copy-done.2, f32[128,128]{1,0:T(8,128)S(1)} %copy-done.1, f32[256,256]{1,0:T(8,128)S(1)} %get-tuple-element.67.refs_4_, ...), custom_call_target="tpu_custom_call" | custom-call | tf_op jit(solution)/shard_map/spectral_krylov_2/pallas_call | solution.py:427
  151.6 9.4 %all_to_all.92 = f32[32,1,128]{2,1,0:T(1,128)S(1)} all-to-all(f32[32,1,128]{2,1,0:T(1,128)S(1)} %bitcast.61), channel_id=1, replica_groups=mesh['modes'=8,'cheb'=4] {'modes','cheb'}, dimensions={0} | all-to-all | bytes 32768 | tf_op jit(solution)/shard_map/all_to_all | solution.py:486
  161.0 1.1 points_restart_3.1
  162.1 12.3 %all_to_all.93.refs_0_ = f32[32,16,128]{2,1,0:T(8,128)S(1)} all-to-all(f32[32,16,128]{2,1,0:T(8,128)S(1)} %bitcast.52), channel_id=1, replica_groups=mesh['modes'=8,'cheb'=4] {'modes','cheb'}, dimensions={0} | all-to-all | bytes 524288 | tf_op jit(solution)/shard_map/all_to_all | solution.py:486
  174.4 6.3 %spectral_residual_3.1 = (f32[256,256]{1,0:T(8,128)S(1)}, f32[256,256]{1,0:T(8,128)S(1)}, f32[544,128]{1,0:T(8,128)S(1)}) custom-call(f32[32,16,128]{2,1,0:T(8,128)S(1)} %all_to_all.93.refs_0_, bf16[2,256,256]{2,1,0:T(8,128)(2,1)S(1)} %copy-done, bf16[2,256,256]{2,1,0:T(8,128)(2,1)S(1)} %copy-done.2, f32[128,128]{1,0:T(8,128)S(1)} %copy-done.1, ...), custom_call_target="tpu_custom_call" | custom-call | tf_op jit(solution)/shard_map/spectral_residual_3/pallas_call | solution.py:427
  180.7 13.2 %all_to_all.94 = f32[32,1,2176]{2,1,0:T(1,128)S(1)} all-to-all(f32[32,1,2176]{2,1,0:T(1,128)S(1)} %bitcast.45), channel_id=1, replica_groups=mesh['modes'=8,'cheb'=4] {'modes','cheb'}, dimensions={0} | all-to-all | bytes 557056 | tf_op jit(solution)/shard_map/all_to_all | solution.py:486
  193.9 2.2 points_basis_0.3
  196.1 12.6 %all_to_all.95.refs_0_ = f32[32,16,128]{2,1,0:T(8,128)S(1)} all-to-all(f32[32,16,128]{2,1,0:T(8,128)S(1)} %bitcast.56), channel_id=1, replica_groups=mesh['modes'=8,'cheb'=4] {'modes','cheb'}, dimensions={0} | all-to-all | bytes 524288 | tf_op jit(solution)/shard_map/all_to_all | solution.py:486
  208.7 6.3 %spectral_krylov_0.3 = (f32[256,256]{1,0:T(8,128)S(1)}, f32[256,256]{1,0:T(8,128)S(1)}, f32[544,128]{1,0:T(8,128)S(1)}) custom-call(f32[32,16,128]{2,1,0:T(8,128)S(1)} %all_to_all.95.refs_0_, bf16[2,256,256]{2,1,0:T(8,128)(2,1)S(1)} %copy-done, bf16[2,256,256]{2,1,0:T(8,128)(2,1)S(1)} %copy-done.2, f32[128,128]{1,0:T(8,128)S(1)} %copy-done.1, ...), custom_call_target="tpu_custom_call" | custom-call | tf_op jit(solution)/shard_map/spectral_krylov_0/pallas_call | solution.py:427
  215.0 13.3 %all_to_all.96 = f32[32,1,2176]{2,1,0:T(1,128)S(1)} all-to-all(f32[32,1,2176]{2,1,0:T(1,128)S(1)} %bitcast.49), channel_id=1, replica_groups=mesh['modes'=8,'cheb'=4] {'modes','cheb'}, dimensions={0} | all-to-all | bytes 557056 | tf_op jit(solution)/shard_map/all_to_all | solution.py:486
  228.3 2.2 points_basis_1.3
  230.5 12.6 %all_to_all.97.refs_0_ = f32[32,16,128]{2,1,0:T(8,128)S(1)} all-to-all(f32[32,16,128]{2,1,0:T(8,128)S(1)} %bitcast.57), channel_id=1, replica_groups=mesh['modes'=8,'cheb'=4] {'modes','cheb'}, dimensions={0} | all-to-all | bytes 524288 | tf_op jit(solution)/shard_map/all_to_all | solution.py:486
  243.1 6.3 %spectral_krylov_1.3 = (f32[256,256]{1,0:T(8,128)S(1)}, f32[256,256]{1,0:T(8,128)S(1)}, f32[544,128]{1,0:T(8,128)S(1)}) custom-call(f32[32,16,128]{2,1,0:T(8,128)S(1)} %all_to_all.97.refs_0_, bf16[2,256,256]{2,1,0:T(8,128)(2,1)S(1)} %copy-done, bf16[2,256,256]{2,1,0:T(8,128)(2,1)S(1)} %copy-done.2, f32[128,128]{1,0:T(8,128)S(1)} %copy-done.1, ...), custom_call_target="tpu_custom_call" | custom-call | tf_op jit(solution)/shard_map/spectral_krylov_1/pallas_call | solution.py:427
  249.4 13.3 %all_to_all.98 = f32[32,1,2176]{2,1,0:T(1,128)S(1)} all-to-all(f32[32,1,2176]{2,1,0:T(1,128)S(1)} %bitcast.50), channel_id=1, replica_groups=mesh['modes'=8,'cheb'=4] {'modes','cheb'}, dimensions={0} | all-to-all | bytes 557056 | tf_op jit(solution)/shard_map/all_to_all | solution.py:486
  262.7 2.7 points_basis_2.3
  265.4 12.6 %all_to_all.99.refs_0_ = f32[32,16,128]{2,1,0:T(8,128)S(1)} all-to-all(f32[32,16,128]{2,1,0:T(8,128)S(1)} %bitcast.51), channel_id=1, replica_groups=mesh['modes'=8,'cheb'=4] {'modes','cheb'}, dimensions={0} | all-to-all | bytes 524288 | tf_op jit(solution)/shard_map/all_to_all | solution.py:486
  278.0 6.1 %spectral_krylov_2.3 = (f32[256,256]{1,0:T(8,128)S(1)}, f32[32,128]{1,0:T(8,128)S(1)}) custom-call(f32[32,16,128]{2,1,0:T(8,128)S(1)} %all_to_all.99.refs_0_, bf16[2,256,256]{2,1,0:T(8,128)(2,1)S(1)} %copy-done, bf16[2,256,256]{2,1,0:T(8,128)(2,1)S(1)} %copy-done.2, f32[128,128]{1,0:T(8,128)S(1)} %copy-done.1, f32[256,256]{1,0:T(8,128)S(1)} %get-tuple-element.89.refs_4_, ...), custom_call_target="tpu_custom_call" | custom-call | tf_op jit(solution)/shard_map/spectral_krylov_2/pallas_call | solution.py:427
  284.2 9.4 %all_to_all.100 = f32[32,1,128]{2,1,0:T(1,128)S(1)} all-to-all(f32[32,1,128]{2,1,0:T(1,128)S(1)} %bitcast.60), channel_id=1, replica_groups=mesh['modes'=8,'cheb'=4] {'modes','cheb'}, dimensions={0} | all-to-all | bytes 32768 | tf_op jit(solution)/shard_map/all_to_all | solution.py:486
  293.6 0.3 finish.1
  293.9 0.1 copy.40
  294.0 0.7 copy.41
  (12 shorter events, 0.0 us)
Async XLA Ops:
  24.0 13.2 %all-to-all-start.1 = ((f32[32,16,128]{2,1,0:T(8,128)}), f32[32,16,128]{2,1,0:T(8,128)S(1)}, u32[]{:S(2)}, u32[]{:S(2)}) async-start(f32[32,16,128]{2,1,0:T(8,128)} %bitcast.3), calls=%async_computation.1 | async-start | bytes 524288 | tf_op jit(solution)/shard_map/all_to_all | solution.py:486
  27.7 34.1 %copy-start.1 = (f32[128,128]{1,0:T(8,128)S(1)}, f32[128,128]{1,0:T(8,128)}, u32[]{:S(2)}) copy-start(f32[128,128]{1,0:T(8,128)} %constant.25.clone.refs_6_.refs_3_.refs_1_) | copy-start | bytes 196612
  27.7 34.1 %copy-start.3 = (bf16[2,128,256]{2,1,0:T(8,128)(2,1)S(1)}, bf16[2,128,256]{2,1,0:T(8,128)(2,1)}, u32[]{:S(2)}) copy-start(bf16[2,128,256]{2,1,0:T(8,128)(2,1)} %constant.23.clone.refs_4_) | copy-start | bytes 393220
  27.7 34.1 %copy-start.4 = (bf16[2,256,128]{2,1,0:T(8,128)(2,1)S(1)}, bf16[2,256,128]{2,1,0:T(8,128)(2,1)}, u32[]{:S(2)}) copy-start(bf16[2,256,128]{2,1,0:T(8,128)(2,1)} %constant.22.clone.refs_3_) | copy-start | bytes 393220
  27.7 34.1 %copy-start.5 = (bf16[2,256,64]{2,1,0:T(8,128)(2,1)S(1)}, bf16[2,256,64]{2,1,0:T(8,128)(2,1)}, u32[]{:S(2)}) copy-start(bf16[2,256,64]{2,1,0:T(8,128)(2,1)} %constant.19.clone.refs_0_) | copy-start | bytes 196612
  27.7 34.1 %copy-start.6 = (f32[3,64,128]{2,1,0:T(8,128)S(1)}, f32[3,64,128]{2,1,0:T(8,128)}, u32[]{:S(2)}) copy-start(f32[3,64,128]{2,1,0:T(8,128)} %constant.20.clone.refs_1_) | copy-start | bytes 294916
  27.7 34.1 %copy-start.7 = (bf16[2,64,128]{2,1,0:T(8,128)(2,1)S(1)}, bf16[2,64,128]{2,1,0:T(8,128)(2,1)}, u32[]{:S(2)}) copy-start(bf16[2,64,128]{2,1,0:T(8,128)(2,1)} %constant.24.clone.refs_5_) | copy-start | bytes 98308
  27.7 34.1 %copy-start.8 = (f32[64,128]{1,0:T(8,128)S(1)}, f32[64,128]{1,0:T(8,128)}, u32[]{:S(2)}) copy-start(f32[64,128]{1,0:T(8,128)} %constant.21.clone.refs_2_) | copy-start | bytes 98308
  27.8 48.9 %copy-start = (bf16[2,256,256]{2,1,0:T(8,128)(2,1)S(1)}, bf16[2,256,256]{2,1,0:T(8,128)(2,1)}, u32[]{:S(2)}) copy-start(bf16[2,256,256]{2,1,0:T(8,128)(2,1)} %constant.18.clone.ct.refs_1_) | copy-start | bytes 786436
  27.8 48.9 %copy-start.2 = (bf16[2,256,256]{2,1,0:T(8,128)(2,1)S(1)}, bf16[2,256,256]{2,1,0:T(8,128)(2,1)}, u32[]{:S(2)}) copy-start(bf16[2,256,256]{2,1,0:T(8,128)(2,1)} %constant.26.clone.refs_2_) | copy-start | bytes 786436
